TPU v7x, 32 devices: a whole 2x2x4 slice. The times are simulated.
32 devices in a mesh: ea: 8 (over z, y), ba: 4 (over x, core).
Axes of the slice: x: 2, y: 2, z: 4, core: 2. Of those that a mesh axis runs over, the one named last changes fastest.
Arguments:
- entities: float32 [4096, 200], P('ea'), may hold values from -1.5 to 1.5
- entity_history: float32 [4096], P('ea'), may hold values from 0.001 to 0.1
- relations: float32 [256, 200], replicated, may hold values from -6 to 6
- relation_history: float32 [256], replicated, may hold values from 0.001 to 0.1
- edge_ends: int32 [8192, 2], P(('ba', 'ea')), may hold values from 0 to 4095, as said below
- edge_relations: int32 [8192], P(('ba', 'ea')), may hold values from 0 to 255
- negatives: int32 [8192], P(('ba', 'ea')), may hold values from 0 to 4095, as said below
Outputs:
- entity_step: float32 [4096, 200], P('ea')
- entity_squares: float32 [4096], P('ea')
- relation_step: float32 [256, 200], replicated
- relation_squares: float32 [256], replicated
- mean_loss: float32 [1], replicated
Inputs may be any that keep to these rules, and one draw needn't show every extreme that they name: `edge_ends`: every entry is an entity id. In each aligned block of 256 edges at most 48 heads have the same owner shard (id // 512), and some shard has exactly 48; the same holds for the tails. Every entry is an entity id. In each run of 256 consecutive negatives at most 48 have the same owner shard (id // 512), and some shard has exactly 48. `edge_relations`: every entry is a relation id.
All inputs are finite; a program needn't handle non-finite values.
Results may differ from a plain program's by a relative error of at most 0.0003.
Values sent between devices are 32-bit elements.
A program may use at most 64 MiB of HBM per device.

v0:
```python
import jax
import jax.numpy as jnp
from jax import lax
from jax.sharding import PartitionSpec as P

learn_rate = 0.1
adagrad_eps = 1e-10
highest = lax.Precision.HIGHEST


def halves(vectors):
    half_width = vectors.shape[-1] // 2
    return (vectors[..., :half_width], vectors[..., half_width:])


def complex_times(former, latter):
    former_real, former_imag = halves(former)
    latter_real, latter_imag = halves(latter)
    return jnp.concatenate(
        [
            former_real * latter_real - former_imag * latter_imag,
            former_real * latter_imag + former_imag * latter_real,
        ],
        axis=-1,
    )


def conjugate(vectors):
    real_part, imag_part = halves(vectors)
    return jnp.concatenate([real_part, -imag_part], axis=-1)


def adagrad_step(slope_vector, history):
    squares = history + jnp.mean(slope_vector * slope_vector, axis=1)
    return (-learn_rate * slope_vector / (jnp.sqrt(squares)[:, None] + adagrad_eps), squares)


def bucket_slots(node_labels, shard_rows, peer_count, room_limit):
    owners = node_labels // shard_rows
    local_rows = node_labels - owners * shard_rows
    onehot = (owners[:, None] == jnp.arange(peer_count, dtype=jnp.int32)[None, :]).astype(jnp.int32)
    earlier = jnp.cumsum(onehot, axis=0) - onehot
    slot_positions = owners * room_limit + jnp.sum(earlier * onehot, axis=1)
    request = jnp.full((peer_count * room_limit,), -1, jnp.int32).at[slot_positions].set(local_rows)
    return (slot_positions, request.reshape(peer_count, room_limit))


def serve_rows(table, demanded_lookups):
    picked = jnp.take(table, jnp.maximum(demanded_lookups, 0), axis=0)
    return jnp.where((demanded_lookups >= 0)[..., None], picked, 0.0)


def outgoing_rows(slope_vector, slot_positions, peer_count, room_limit):
    buffer_rows = (
        jnp.zeros((peer_count * room_limit, slope_vector.shape[1]), jnp.float32)
        .at[slot_positions]
        .set(slope_vector)
    )
    return buffer_rows.reshape(peer_count, room_limit, slope_vector.shape[1])


def absorb(dense_grad, demanded_lookups, incoming):
    flat_rows = jnp.maximum(demanded_lookups, 0).reshape(-1)
    return dense_grad.at[flat_rows].add(incoming.reshape(-1, incoming.shape[-1]))


def matmul(former, latter):
    return jnp.dot(former, latter, precision=highest, preferred_element_type=jnp.float32)


def spread_back(weights, probe_rows):
    return lax.dot_general(
        weights,
        probe_rows,
        (((0,), (0,)), ((), ())),
        precision=highest,
        preferred_element_type=jnp.float32,
    )


def side_terms(probe_rows, positive, candidates):
    scores = lax.dot_general(
        probe_rows,
        candidates,
        (((1,), (1,)), ((), ())),
        precision=highest,
        preferred_element_type=jnp.float32,
    )
    own_edge = lax.broadcasted_iota(jnp.int32, scores.shape, 1) == lax.broadcasted_iota(
        jnp.int32, scores.shape, 0
    )
    scores = jnp.where(own_edge, -jnp.inf, scores)
    peak = jnp.maximum(jnp.max(scores, axis=1), positive)
    lifted = jnp.exp(scores - peak[:, None])
    struck = jnp.exp(positive - peak)
    normal = struck + jnp.sum(lifted, axis=1)
    loss_sum = jnp.sum(jnp.log(normal) + peak - positive)
    return (loss_sum, lifted / normal[:, None], struck / normal)


def on_device(
    entities, entity_history, relations, relation_history, edge_ends, edge_relations, negatives
):
    peer_count = lax.axis_size("ea")
    shard_rows = entities.shape[0]
    row_width = entities.shape[1]
    edge_count = edge_ends.shape[0]
    negative_count = negatives.shape[0]
    edge_share = edge_count // peer_count
    link_room = edge_share + max(1, edge_share // 2)
    negative_share = negative_count // peer_count
    contrast_room = negative_share + max(1, negative_share // 2)
    desired_items = (edge_ends[:, 0], edge_ends[:, 1], negatives)
    room_limits = (link_room, link_room, contrast_room)
    joint_capacity = sum(room_limits)
    joint_places, joint_request = bucket_slots(
        jnp.concatenate(desired_items), shard_rows, peer_count, joint_capacity
    )
    joint_asked = lax.all_to_all(joint_request, "ea", split_axis=0, concat_axis=0, tiled=True)
    joint_answer = lax.all_to_all(
        serve_rows(entities, joint_asked), "ea", split_axis=0, concat_axis=0, tiled=True
    )
    fetched = joint_answer.reshape(-1, row_width)[joint_places]
    head_rows = fetched[:edge_count]
    tail_rows = fetched[edge_count : 2 * edge_count]
    negative_rows = fetched[2 * edge_count :]
    related = jnp.take(relations, edge_relations, axis=0)
    tail_query = complex_times(head_rows, related)
    head_probe = complex_times(conjugate(related), tail_rows)
    positive = jnp.sum(tail_query * tail_rows, axis=1)
    tail_cands = jnp.concatenate([tail_rows, negative_rows], axis=0)
    head_cands = jnp.concatenate([head_rows, negative_rows], axis=0)
    tail_loss, tail_weight, tail_struck = side_terms(tail_query, positive, tail_cands)
    head_loss, head_weight, head_struck = side_terms(head_probe, positive, head_cands)
    gain = tail_struck + head_struck - 2.0
    tail_back = matmul(tail_weight, tail_cands) + gain[:, None] * tail_rows
    head_back = matmul(head_weight, head_cands)
    tail_spread = spread_back(tail_weight, tail_query)
    head_spread = spread_back(head_weight, head_probe)
    head_grad = complex_times(tail_back, conjugate(related)) + head_spread[:edge_count]
    tail_grad = (
        gain[:, None] * tail_query + complex_times(head_back, related) + tail_spread[:edge_count]
    )
    negative_grad = tail_spread[edge_count:] + head_spread[edge_count:]
    relation_rows = complex_times(tail_back, conjugate(head_rows)) + complex_times(
        conjugate(head_back), tail_rows
    )
    relation_local = jax.ops.segment_sum(
        relation_rows, edge_relations, num_segments=relations.shape[0]
    )
    loss_local = tail_loss + head_loss
    dense_grad = jnp.zeros((shard_rows, row_width), jnp.float32)
    joint_grad = jnp.concatenate([head_grad, tail_grad, negative_grad], axis=0)
    incoming = lax.all_to_all(
        outgoing_rows(joint_grad, joint_places, peer_count, joint_capacity),
        "ea",
        split_axis=0,
        concat_axis=0,
        tiled=True,
    )
    dense_grad = absorb(dense_grad, joint_asked, incoming)
    relation_sum, loss_sum = lax.psum((relation_local, loss_local), ("ea", "ba"))
    relation_step, relation_squares = adagrad_step(relation_sum, relation_history)
    mean_loss = (loss_sum / (2.0 * edge_count * peer_count * lax.axis_size("ba"))).reshape(1)
    summed = lax.psum(dense_grad, "ba")
    entity_step, entity_squares = adagrad_step(summed, entity_history)
    return (entity_step, entity_squares, relation_step, relation_squares, mean_loss)


def solution(mesh):
    placed = (
        P("ea", None),
        P("ea"),
        P(),
        P(),
        P(("ba", "ea"), None),
        P(("ba", "ea")),
        P(("ba", "ea")),
    )
    return jax.shard_map(
        on_device,
        mesh=mesh,
        in_specs=placed,
        out_specs=(P("ea", None), P("ea"), P(), P(), P()),
        check_vma=False,
    )
```

profile of v0, /device:TPU:1, one launch (start us, length us, event | category | flops | bytes accessed | tf_op | source)
XLA Modules:
  0.0 281.8 jit_solution(15245476762388330828)
XLA Ops:
  8.0 0.8 fusion.40
  9.5 1.7 reduce-window.6
  11.7 0.7 multiply_subtract_fusion.6
  12.4 0.7 fusion.25
  13.2 3.4 %scatter_custom_fusion = s32[1152]{0:T(1024)S(1)} fusion(s32[768]{0:T(1024)S(1)} %fusion.25, s32[768]{0:T(1024)S(1)} %get-tuple-element.59, s32[]{:T(128)} %constant.34.clone.1), kind=kCustom, calls=%fused_computation.89 | custom fusion | bytes 4612 | tf_op jit(solution)/shard_map/scatter | solution.py:44
  17.2 6.4 %all-to-all-start = ((s32[8,1,144]{2,1,0:T(1,128)}), s32[8,1,144]{2,1,0:T(1,128)S(1)}, u32[]{:S(2)}, u32[]{:S(2)}) async-start(s32[8,1,144]{2,1,0:T(1,128)} %all_to_all.12), calls=%async_computation | async-start | bytes 16384 | tf_op jit(solution)/shard_map/all_to_all | solution.py:119
  23.6 1.2 copy.54
  24.8 4.2 %all-to-all-done = s32[8,1,144]{2,1,0:T(1,128)S(1)} async-done(((s32[8,1,144]{2,1,0:T(1,128)}), s32[8,1,144]{2,1,0:T(1,128)S(1)}, u32[]{:S(2)}, u32[]{:S(2)}) %all-to-all-start) | async-done | bytes 4640 | tf_op jit(solution)/shard_map/all_to_all | solution.py:119
  29.1 3.3 %gather_fusion = f32[1152,200]{1,0:T(8,128)S(1)} fusion(f32[512,200]{1,0:T(8,128)S(1)} %copy.54, s32[2048]{0:T(1024)S(1)} %pad_clamp_fusion), kind=kCustom, calls=%fused_computation | custom fusion | bytes 1847808 | tf_op jit(solution)/shard_map/jit(_take)/gather | solution.py:49
  32.4 1.3 select_select_fusion
  33.7 3.9 %all-to-all-start.1 = ((f32[8,144,200]{2,1,0:T(8,128)}), f32[8,144,200]{2,1,0:T(8,128)S(1)}, u32[]{:S(2)}, u32[]{:S(2)}) async-start(f32[8,144,200]{2,1,0:T(8,128)} %select_select_fusion), calls=%async_computation.1 | async-start | bytes 2359296 | tf_op jit(solution)/shard_map/all_to_all | solution.py:120
  37.8 1.0 gather_fusion.2
  39.0 25.6 %all-to-all-done.1 = f32[8,144,200]{2,1,0:T(8,128)S(1)} async-done(((f32[8,144,200]{2,1,0:T(8,128)}), f32[8,144,200]{2,1,0:T(8,128)S(1)}, u32[]{:S(2)}, u32[]{:S(2)}) %all-to-all-start.1) | async-done | bytes 921632 | tf_op jit(solution)/shard_map/all_to_all | solution.py:120
  64.6 2.1 gather_fusion.1
  67.5 1.2 fusion.43
  68.8 1.2 fusion.42
  70.9 1.1 fusion.8
  72.0 0.7 fusion.11
  72.7 0.7 fusion.14
  73.4 1.1 convolution_add_fusion
  75.2 6.6 %scatter_custom_fusion.1 = f32[1152,200]{1,0:T(8,128)} fusion(s32[768]{0:T(1024)S(1)} %fusion.25, f32[768,200]{1,0:T(8,128)S(1)} %copy.62, f32[]{:T(128)} %constant.33.clone.1), kind=kCustom, calls=%fused_computation.12 | custom fusion | bytes 921604 | tf_op jit(solution)/shard_map/scatter | solution.py:57
  81.7 5.6 %all-to-all-start.2 = ((f32[8,144,200]{2,1,0:T(8,128)}), f32[8,144,200]{2,1,0:T(8,128)S(1)}, u32[]{:S(2)}, u32[]{:S(2)}) async-start(f32[8,144,200]{2,1,0:T(8,128)} %bitcast.10), calls=%async_computation.2 | async-start | bytes 2359296 | tf_op jit(solution)/shard_map/all_to_all | solution.py:154
  87.8 2.6 scatter_custom_fusion.3
  91.8 45.3 %psum.23 = f32[]{:T(128)} all-reduce(f32[]{:T(128)S(6)} %add.183), channel_id=1, replica_groups=mesh['ea'=8,'ba'=4] {'ea','ba'}, use_global_device_ids=true, to_apply=%region_18.19 | all-reduce | flops 1 | bytes 8 | tf_op jit(solution)/shard_map/psum | solution.py:162
  137.7 88.9 %all-reduce.5.cloned.1.call-done = f32[256,200]{1,0:T(8,128)} async-done(((f32[256,200]{1,0:T(8,128)}), f32[256,200]{1,0:T(8,128)}) %all-reduce.5.cloned.1.call-update) | async-done | bytes 204816 | tf_op jit(solution)/shard_map/psum | solution.py:162
  226.6 1.1 multiply_reduce_fusion.1
  228.3 9.5 %scatter_custom_fusion.2 = f32[512,200]{1,0:T(8,128)} fusion(s32[1152]{0:T(1024)S(1)} %reshape.425, f32[1152,200]{1,0:T(8,128)S(1)} %bitcast.44, f32[]{:T(128)} %constant.33.clone.1), kind=kCustom, calls=%fused_computation.29 | custom fusion | flops 230400 | bytes 409604 | tf_op jit(solution)/shard_map/scatter-add | solution.py:64
  237.9 0.8 copy.65
  238.7 30.6 %all-reduce.3.cloned.1.call-done = f32[512,200]{1,0:T(8,128)} async-done(((f32[512,200]{1,0:T(8,128)}), f32[512,200]{1,0:T(8,128)}) %all-reduce.3.cloned.1.call-update) | async-done | bytes 409616 | tf_op jit(solution)/shard_map/psum | solution.py:165
  269.3 1.2 multiply_reduce_fusion
  271.1 1.2 multiply_divide_fusion
  272.3 0.9 copy.64
  (57 shorter events, 6.5 us)
Async XLA Ops:
  17.2 11.8 %all-to-all-start = ((s32[8,1,144]{2,1,0:T(1,128)}), s32[8,1,144]{2,1,0:T(1,128)S(1)}, u32[]{:S(2)}, u32[]{:S(2)}) async-start(s32[8,1,144]{2,1,0:T(1,128)} %all_to_all.12), calls=%async_computation | async-start | bytes 16384 | tf_op jit(solution)/shard_map/all_to_all | solution.py:119
  33.7 3.9 %copy-start.1 = (f32[256,200]{0,1:T(8,128)S(1)}, f32[256,200]{0,1:T(8,128)}, u32[]{:S(2)}) copy-start(f32[256,200]{0,1:T(8,128)} %param.9) | copy-start | bytes 614404
  33.7 4.0 %copy-start.3 = (s32[256]{0:T(256)S(1)}, s32[256]{0:T(256)}, u32[]{:S(2)}) copy-start(s32[256]{0:T(256)} %param.12) | copy-start | bytes 3076
  33.7 30.8 %all-to-all-start.1 = ((f32[8,144,200]{2,1,0:T(8,128)}), f32[8,144,200]{2,1,0:T(8,128)S(1)}, u32[]{:S(2)}, u32[]{:S(2)}) async-start(f32[8,144,200]{2,1,0:T(8,128)} %select_select_fusion), calls=%async_computation.1 | async-start | bytes 2359296 | tf_op jit(solution)/shard_map/all_to_all | solution.py:120
  81.7 146.6 %all-to-all-start.2 = ((f32[8,144,200]{2,1,0:T(8,128)}), f32[8,144,200]{2,1,0:T(8,128)S(1)}, u32[]{:S(2)}, u32[]{:S(2)}) async-start(f32[8,144,200]{2,1,0:T(8,128)} %bitcast.10), calls=%async_computation.2 | async-start | bytes 2359296 | tf_op jit(solution)/shard_map/all_to_all | solution.py:154
  87.3 140.4 %copy-start.4 = (f32[256]{0:T(256)S(1)}, f32[256]{0:T(256)}, u32[]{:S(2)}) copy-start(f32[256]{0:T(256)} %param.10) | copy-start | bytes 3076
  87.3 139.3 %all-reduce.5.cloned.1.call-start = ((), (), s32[]{:S(2)}) async-start(), calls=%async_computation.4 | async-start | bytes 524288 | tf_op jit(solution)/shard_map/psum | solution.py:162
  90.4 178.9 %all-reduce.3.cloned.1.call-start = ((), (), s32[]{:S(2)}) async-start(), calls=%async_computation.3 | async-start | bytes 1048576 | tf_op jit(solution)/shard_map/psum | solution.py:165
  226.6 11.2 %copy-start = (f32[256,200]{1,0:T(8,128)S(1)}, f32[256,200]{1,0:T(8,128)}, u32[]{:S(2)}) copy-start(f32[256,200]{1,0:T(8,128)} %all-reduce.5.cloned.1.call-done) | copy-start | bytes 614404
  228.3 42.2 %copy-start.2 = (f32[512]{0:T(512)S(1)}, f32[512]{0:T(512)}, u32[]{:S(2)}) copy-start(f32[512]{0:T(512)} %param.8) | copy-start | bytes 6148
Sparse Core Ops, SparseCore 0:
  94.2 132.3 all-reduce.4
Sparse Core Ops, SparseCore 1:
  237.9 31.4 all-reduce.2
where the time goes:
time: 285 us; the launch traced here: 282 us
  waiting for transfers between devices  149 us (52%)
  blocking collectives  45.3 us (16%)
  other arithmetic  23.7 us (8%)
  local copies, waits for them, and re-layouts  22.4 us (8%)
  between operations  18.9 us (7%)
  starting transfers between devices  16.2 us (6%)
  matrix products  5.94 us (2%)
    psum x1, waiting for transfers between devices, on_device(): lax.psum((relation_local, loss_local), ('ea', 'ba'))  88.9 us
    psum x1, blocking collectives, on_device(): lax.psum((relation_local, loss_local), ('ea', 'ba'))  45.3 us
    psum x1, waiting for transfers between devices, on_device(): summed = lax.psum(dense_grad, 'ba')  30.6 us
    all_to_all x1, waiting for transfers between devices, on_device(): lax.all_to_all(serve_rows(entities, joint_asked), 'ea', split_axis=0, con...  25.6 us
    scatter-add x1, other arithmetic, absorb(): dense_grad.at[flat_rows].add(incoming.reshape(-1, incoming.shape[-1]))  9.45 us
    scatter x1, local copies, waits for them, and re-layouts, outgoing_rows(): buffer_rows = jnp.zeros((peer_count * room_limit, slope_vector.shape[1]),...  6.55 us
    all_to_all x1, starting transfers between devices, on_device(): lax.all_to_all(joint_request, 'ea', split_axis=0, concat_axis=0, tiled=True)  6.38 us
  transfers between devices with their start and end apart: 5, of which 4 were waited for; matrix products, arithmetic and copies ran while one was open for 3% of the time, Pallas kernels for 0%

commit v1 on v0

--- a/solution.py
+++ b/solution.py
@@ -1,6 +1,10 @@
+import functools
+
 import jax
 import jax.numpy as jnp
 from jax import lax
+from jax.experimental import pallas as pl
+from jax.experimental.pallas import tpu as pltpu
 from jax.sharding import PartitionSpec as P
 
 learn_rate = 0.1
@@ -167,6 +171,394 @@
     return (entity_step, entity_squares, relation_step, relation_squares, mean_loss)
 
 
+LANES = 128
+TAIL_ROWS = 16
+MESH = pl.DeviceIdType.MESH
+f32 = jnp.float32
+
+
+def split_two(values):
+    upper = values.astype(jnp.bfloat16)
+    return upper, (values - upper.astype(f32)).astype(jnp.bfloat16)
+
+
+def dot_of(former, latter, dims):
+    return lax.dot_general(former, latter, (dims, ((), ())), preferred_element_type=f32)
+
+
+def dot_three(former, latter, dims):
+    return dot_of(former[0], latter[0], dims) + (
+        dot_of(former[0], latter[1], dims) + dot_of(former[1], latter[0], dims)
+    )
+
+
+def pick_rows(onehot, halves_of):
+    dims = ((1,), (0,))
+    return dot_of(onehot, halves_of[0], dims) + dot_of(onehot, halves_of[1], dims)
+
+
+def times(former, latter):
+    a, b = former[:, :LANES], former[:, LANES:]
+    c, d = latter[:, :LANES], latter[:, LANES:]
+    return jnp.concatenate([a * c - b * d, a * d + b * c], axis=1)
+
+
+def times_conj(former, latter):
+    a, b = former[:, :LANES], former[:, LANES:]
+    c, d = latter[:, :LANES], latter[:, LANES:]
+    return jnp.concatenate([a * c + b * d, b * c - a * d], axis=1)
+
+
+def one_side(probe, positive, cands):
+    probe_parts, cand_parts = split_two(probe), split_two(cands)
+    scores = dot_three(probe_parts, cand_parts, ((1,), (1,)))
+    own = lax.broadcasted_iota(jnp.int32, scores.shape, 1) == lax.broadcasted_iota(
+        jnp.int32, scores.shape, 0
+    )
+    scores = jnp.where(own, -jnp.inf, scores)
+    peak = jnp.maximum(jnp.max(scores, axis=1, keepdims=True), positive)
+    lifted = jnp.exp(scores - peak)
+    struck = jnp.exp(positive - peak)
+    normal = struck + jnp.sum(lifted, axis=1, keepdims=True)
+    loss = jnp.sum(jnp.log(normal) + peak - positive, axis=0, keepdims=True)
+    weight = split_two(lifted / normal)
+    back = dot_three(weight, cand_parts, ((1,), (0,)))
+    spread = dot_three(weight, probe_parts, ((0,), (0,)))
+    return loss, struck / normal, back, spread
+
+
+def step_kernel(
+    n,
+    ids_col,
+    ids_row,
+    kinds_col,
+    kinds_row,
+    ent,
+    rels,
+    sum_out,
+    rel_out,
+    loss_out,
+    tab,
+    rows,
+    grad_hi,
+    grad_lo,
+    rel_local,
+    loss_local,
+    pbuf,
+    dbuf,
+    rbuf,
+    fin,
+    xbuf,
+    full,
+    relbuf,
+    ag_send,
+    ag_recv,
+    pair_send,
+    pair_recv,
+    rs_send,
+    rs_recv,
+    half_send,
+    half_recv,
+    last_send,
+    last_recv,
+    rel_send,
+    rel_recv,
+):
+    mid = n // 2
+    shard = ent.shape[0]
+    edges = kinds_col.shape[0]
+    reads = ids_col.shape[0]
+    rel_share = rels.shape[0] // n
+    chunk = pbuf.shape[1]
+    me = lax.axis_index("ea")
+    lane = lax.axis_index("ba")
+    core = lax.rem(lane, 2)
+
+    def at(place):
+        place = lax.rem(place + 2 * n, n)
+        return 2 * place + (place // mid) * (2 * (n - place) - 1 - 2 * place)
+
+    high, odd = me // 2, lax.rem(me, 2)
+    pos = high + odd * (n - 1 - 2 * high)
+    onward = ({"ea": at(pos + 1)}, {"ea": at(pos - 1)})
+    partner = {"ba": lane + 1 - 2 * core}
+    across = {"ba": lax.rem(lane + 2, 4)}
+
+    barrier = pltpu.get_barrier_semaphore()
+    for j in range(1, n):
+        pl.semaphore_signal(barrier, inc=1, device_id={"ea": lax.rem(me + j, n)}, device_id_type=MESH)
+    pl.semaphore_signal(barrier, inc=1, device_id=partner, device_id_type=MESH)
+    pl.semaphore_signal(barrier, inc=1, device_id=across, device_id_type=MESH)
+    pl.semaphore_wait(barrier, n + 1)
+
+    sent = []
+
+    def send(src, dst, send_sem, recv_sem, device):
+        return pltpu.make_async_remote_copy(
+            src_ref=src, dst_ref=dst, send_sem=send_sem, recv_sem=recv_sem,
+            device_id=device, device_id_type=MESH,
+        )
+
+    def launch(copy):
+        copy.start()
+        sent.append(copy)
+
+    sub = shard // 4
+
+    def ag_rows(u):
+        return pl.ds(pl.multiple_of(core * (2 * sub) + u * sub, 8), sub)
+
+    def ag_active(d, s, u):
+        return s < mid or (s == mid and u == d)
+
+    def ag_copy(d, s, u):
+        source = (s - 1) if d == 0 else (n - (s - 1)) % n
+        target = s if d == 0 else n - s
+        src = ent.at[ag_rows(u)] if s == 1 else tab.at[source, ag_rows(u)]
+        return send(src, tab.at[target, ag_rows(u)], ag_send.at[d, s - 1, u], ag_recv.at[d, s - 1, u], onward[d])
+
+    def pair_copy(slot, u):
+        return send(tab.at[slot, ag_rows(u)], tab.at[slot, ag_rows(u)], pair_send.at[slot, u], pair_recv.at[slot, u], partner)
+
+    def gather(slot):
+        values = ent[...] if slot == 0 else tab[slot]
+        owner = at(pos - slot)
+        onehot = (ids_col[...] - owner * shard == lax.broadcasted_iota(jnp.int32, (reads, shard), 1)).astype(f32).astype(jnp.bfloat16)
+        picked = pick_rows(onehot, split_two(values))
+        if slot == 0:
+            rows[...] = picked
+        else:
+            rows[...] += picked
+
+    for u in range(2):
+        for d in range(2):
+            launch(ag_copy(d, 1, u if d == 0 else 1 - u))
+    gather(0)
+    kinds = (kinds_col[...] == lax.broadcasted_iota(jnp.int32, (edges, rels.shape[0]), 1)).astype(f32).astype(jnp.bfloat16)
+    related = pick_rows(kinds, split_two(rels[...]))
+    slots_of = lambda s: (s, n - s) if s < mid else (s,)
+    for s in range(1, mid + 1):
+        for v in range(2):
+            for d in range(2):
+                u = v if d == 0 else 1 - v
+                if ag_active(d, s, u):
+                    ag_copy(d, s, u).wait_recv()
+                    if s < mid and ag_active(d, s + 1, u):
+                        launch(ag_copy(d, s + 1, u))
+                    launch(pair_copy(s if d == 0 else n - s, u))
+        if s > 1:
+            for slot in slots_of(s - 1):
+                for u in range(2):
+                    pair_copy(slot, u).wait_recv()
+                gather(slot)
+    for u in range(2):
+        pair_copy(mid, u).wait_recv()
+    gather(mid)
+
+    head, tail, contrast = rows[:edges], rows[edges : 2 * edges], rows[2 * edges :]
+    query = times(head, related)
+    probe = times_conj(tail, related)
+    positive = jnp.sum(query * tail, axis=1, keepdims=True)
+    tail_loss, tail_struck, tail_back, tail_spread = one_side(query, positive, jnp.concatenate([tail, contrast], axis=0))
+    head_loss, head_struck, head_back, head_spread = one_side(probe, positive, jnp.concatenate([head, contrast], axis=0))
+    gain = tail_struck + head_struck - 2.0
+    tail_back = tail_back + gain * tail
+    grads = (
+        times_conj(tail_back, related) + head_spread[:edges],
+        gain * query + times(head_back, related) + tail_spread[:edges],
+        tail_spread[edges:] + head_spread[edges:],
+    )
+    start = 0
+    for part in grads:
+        upper, lower = split_two(part)
+        grad_hi[start : start + part.shape[0]] = upper
+        grad_lo[start : start + part.shape[0]] = lower
+        start += part.shape[0]
+    rel_rows = times_conj(tail_back, head) + times_conj(tail, head_back)
+    kinds_t = (kinds_row[...] == lax.broadcasted_iota(jnp.int32, (rels.shape[0], edges), 0)).astype(f32).astype(jnp.bfloat16)
+    rel_local[...] = pick_rows(kinds_t, split_two(rel_rows))
+    corner = (lax.broadcasted_iota(jnp.int32, loss_local.shape, 0) == 0) & (
+        lax.broadcasted_iota(jnp.int32, loss_local.shape, 1) == 0
+    )
+    loss_local[...] = jnp.where(corner, tail_loss + head_loss, 0.0)
+
+    half = chunk // 2
+    cut = (half // 16) * 8
+    mine = pl.multiple_of(core * half, 8)
+    other = pl.multiple_of((1 - core) * half, 8)
+    spans = ((0, cut), (cut, half - cut))
+
+    def half_copy(k):
+        return send(pbuf.at[k, pl.ds(other, half)], dbuf.at[k], half_send.at[k], half_recv.at[k], partner)
+
+    def contribute(k):
+        owner = at(pos + k)
+        onehot = (ids_row[...] - owner * shard == lax.broadcasted_iota(jnp.int32, (shard, reads), 0)).astype(f32).astype(jnp.bfloat16)
+        pbuf[k, :shard] = pick_rows(onehot, (grad_hi[...], grad_lo[...]))
+        pbuf[k, shard : shard + rel_share] = rel_local[pl.ds(pl.multiple_of(owner * rel_share, 8), rel_share)]
+        pbuf[k, shard + rel_share :] = loss_local[...]
+        launch(half_copy(k))
+
+    def rs_active(d, s, u):
+        return s > 1 or u == d
+
+    def rs_copy(d, s, u):
+        k = (mid + 1 - s) if d == 0 else n - (mid + 1 - s)
+        low, size = spans[u]
+        return send(
+            pbuf.at[k, pl.ds(pl.multiple_of(mine + low, 8), size)],
+            rbuf.at[d, s - 1, pl.ds(low, size)],
+            rs_send.at[d, s - 1, u],
+            rs_recv.at[d, s - 1, u],
+            onward[d],
+        )
+
+    chunks_at = lambda s: (mid,) if s == 1 else (mid + 1 - s, n - (mid + 1 - s)) if s <= mid else (0,)
+    for s in (1, 2):
+        for k in chunks_at(s):
+            contribute(k)
+    for s in range(1, mid + 1):
+        for k in chunks_at(s):
+            half_copy(k).wait_recv()
+        for v in range(2):
+            for d in range(2):
+                u = (1 - d) if v == 0 else d
+                if not rs_active(d, s, u):
+                    continue
+                k = (mid + 1 - s) if d == 0 else n - (mid + 1 - s)
+                low, size = spans[u]
+                here = pl.ds(pl.multiple_of(mine + low, 8), size)
+                total = pbuf[k, here] + dbuf[k, pl.ds(low, size)]
+                if s > 1 and rs_active(d, s - 1, u):
+                    rs_copy(d, s - 1, u).wait_recv()
+                    total = total + rbuf[d, s - 2, pl.ds(low, size)]
+                pbuf[k, here] = total
+                launch(rs_copy(d, s, u))
+        if s + 2 <= mid + 1:
+            for k in chunks_at(s + 2):
+                contribute(k)
+    half_copy(0).wait_recv()
+
+    def last_copy(stage, u):
+        low, size = spans[u]
+        if stage == 0:
+            return send(fin.at[pl.ds(low, size)], xbuf.at[pl.ds(low, size)], last_send.at[0, u], last_recv.at[0, u], across)
+        here = pl.ds(pl.multiple_of(mine + low, 8), size)
+        return send(full.at[here], full.at[here], last_send.at[1, u], last_recv.at[1, u], partner)
+
+    for u in (1, 0):
+        low, size = spans[u]
+        total = pbuf[0, pl.ds(pl.multiple_of(mine + low, 8), size)] + dbuf[0, pl.ds(low, size)]
+        for d in range(2):
+            rs_copy(d, mid, u).wait_recv()
+            total = total + rbuf[d, mid - 1, pl.ds(low, size)]
+        fin[pl.ds(low, size)] = total
+        launch(last_copy(0, u))
+    for u in (1, 0):
+        low, size = spans[u]
+        last_copy(0, u).wait_recv()
+        full[pl.ds(pl.multiple_of(mine + low, 8), size)] = fin[pl.ds(low, size)] + xbuf[pl.ds(low, size)]
+        launch(last_copy(1, u))
+    for u in (1, 0):
+        last_copy(1, u).wait_recv()
+
+    def rel_copy(j):
+        return send(full.at[pl.ds(shard, rel_share)], relbuf.at[j], rel_send.at[j], rel_recv.at[j], {"ea": lax.rem(me + j, n)})
+
+    for j in range(1, n):
+        launch(rel_copy(j))
+    sum_out[...] = full[:shard]
+    loss_out[...] = full[shard + rel_share : shard + rel_share + 8, :LANES]
+    rel_out[pl.ds(pl.multiple_of(me * rel_share, 8), rel_share)] = full[shard : shard + rel_share]
+    for j in range(1, n):
+        rel_copy(j).wait_recv()
+        source = lax.rem(me - j + n, n)
+        rel_out[pl.ds(pl.multiple_of(source * rel_share, 8), rel_share)] = relbuf[j]
+    for copy in sent:
+        copy.wait_send()
+
+
+def spread_halves(values):
+    half = values.shape[1] // 2
+    pad = jnp.zeros((values.shape[0], LANES - half), values.dtype)
+    return jnp.concatenate([values[:, :half], pad, values[:, half:], pad], axis=1)
+
+
+def join_halves(values, width):
+    half = width // 2
+    return jnp.concatenate([values[:, :half], values[:, LANES : LANES + half]], axis=1)
+
+
+def on_ring(entities, entity_history, relations, relation_history, edge_ends, edge_relations, negatives):
+    n = lax.axis_size("ea")
+    shard, width = entities.shape
+    rel_count = relations.shape[0]
+    edges = edge_ends.shape[0]
+    ids = jnp.concatenate([edge_ends[:, 0], edge_ends[:, 1], negatives])
+    reads = ids.shape[0]
+    chunk = shard + rel_count // n + TAIL_ROWS
+    wide = 2 * LANES
+    mid = n // 2
+    dma = pltpu.SemaphoreType.DMA
+    vmem = pl.BlockSpec(memory_space=pltpu.VMEM)
+    summed, rel_sum, loss = pl.pallas_call(
+        functools.partial(step_kernel, n),
+        out_shape=(
+            jax.ShapeDtypeStruct((shard, wide), f32),
+            jax.ShapeDtypeStruct((rel_count, wide), f32),
+            jax.ShapeDtypeStruct((8, LANES), f32),
+        ),
+        in_specs=[vmem] * 6,
+        out_specs=(vmem,) * 3,
+        scratch_shapes=[
+            pltpu.VMEM((n, shard, wide), f32),
+            pltpu.VMEM((reads, wide), f32),
+            pltpu.VMEM((reads, wide), jnp.bfloat16),
+            pltpu.VMEM((reads, wide), jnp.bfloat16),
+            pltpu.VMEM((rel_count, wide), f32),
+            pltpu.VMEM((TAIL_ROWS, wide), f32),
+            pltpu.VMEM((n, chunk, wide), f32),
+            pltpu.VMEM((n, chunk // 2, wide), f32),
+            pltpu.VMEM((2, mid, chunk // 2, wide), f32),
+            pltpu.VMEM((chunk // 2, wide), f32),
+            pltpu.VMEM((chunk // 2, wide), f32),
+            pltpu.VMEM((chunk, wide), f32),
+            pltpu.VMEM((n, rel_count // n, wide), f32),
+            dma((2, mid, 2)),
+            dma((2, mid, 2)),
+            dma((n, 2)),
+            dma((n, 2)),
+            dma((2, mid, 2)),
+            dma((2, mid, 2)),
+            dma((n,)),
+            dma((n,)),
+            dma((2, 2)),
+            dma((2, 2)),
+            dma((n,)),
+            dma((n,)),
+        ],
+        compiler_params=pltpu.CompilerParams(
+            collective_id=0, has_side_effects=True, vmem_limit_bytes=60 * 1024 * 1024
+        ),
+    )(
+        ids[:, None],
+        ids[None, :],
+        edge_relations[:, None],
+        edge_relations[None, :],
+        spread_halves(entities),
+        spread_halves(relations),
+    )
+    relation_step, relation_squares = adagrad_step(join_halves(rel_sum, width), relation_history)
+    entity_step, entity_squares = adagrad_step(join_halves(summed, width), entity_history)
+    mean_loss = (loss[0, 0] / (2.0 * edges * n * lax.axis_size("ba"))).reshape(1)
+    return (entity_step, entity_squares, relation_step, relation_squares, mean_loss)
+
+
+def fits_ring(mesh):
+    n = mesh.shape["ea"]
+    return mesh.shape["ba"] == 4 and n % 2 == 0 and 4 <= n <= 16
+
+
 def solution(mesh):
     placed = (
         P("ea", None),
@@ -178,7 +570,7 @@
         P(("ba", "ea")),
     )
     return jax.shard_map(
-        on_device,
+        on_ring if fits_ring(mesh) else on_device,
         mesh=mesh,
         in_specs=placed,
         out_specs=(P("ea", None), P("ea"), P(), P(), P()),

time: 285 us -> 94.2 us (0.33)
  waiting for transfers between devices: 149 us -> 0 us
  Pallas kernels: 0 us -> 76.7 us
  blocking collectives: 45.3 us -> 0 us
  other arithmetic: 23.7 us -> 4.06 us
  between operations: 18.9 us -> 2.54 us
  starting transfers between devices: 16.2 us -> 0 us
  local copies, waits for them, and re-layouts: 22.4 us -> 10.1 us
  matrix products: 5.94 us -> 0 us
    psum x2 -> x0, waiting for transfers between devices: 119 us -> none  [the longest x1 88.9 us: on_device(): lax.psum((relation_local, loss_local), ('ea', 'ba'))]
    pallas_call x0 -> x1, Pallas kernels: none -> 76.7 us  [on_ring(): pl.pallas_call(functools.partial(step_kernel, n), out_shape=(jax.ShapeDty...]
    psum x1 -> x0, blocking collectives: 45.3 us -> none  [on_device(): lax.psum((relation_local, loss_local), ('ea', 'ba'))]
    all_to_all x3 -> x0, waiting for transfers between devices: 29.8 us -> none  [the longest x1 25.6 us: on_device(): lax.all_to_all(serve_rows(entities, joint_asked), 'ea', split_axis=0, con...]
    all_to_all x3 -> x0, starting transfers between devices: 15.9 us -> none  [the longest x1 6.38 us: on_device(): lax.all_to_all(joint_request, 'ea', split_axis=0, concat_axis=0, tiled=True)]
    scatter-add x2 -> x0, other arithmetic: 12.1 us -> none  [the longest x1 9.45 us: absorb(): dense_grad.at[flat_rows].add(incoming.reshape(-1, incoming.shape[-1]))]
    scatter x2 -> x0, local copies, waits for them, and re-layouts: 9.94 us -> none  [the longest x1 6.55 us: outgoing_rows(): buffer_rows = jnp.zeros((peer_count * room_limit, slope_vector.shape[1]),...]
    gather x4 -> x0, local copies, waits for them, and re-layouts: 6.45 us -> none  [the longest x1 3.27 us: serve_rows(): picked = jnp.take(table, jnp.maximum(demanded_lookups, 0), axis=0)]
  transfers between devices with their start and end apart: 5 -> 0, of which waited for: 4 -> 0; matrix products, arithmetic and copies ran while one was open for 3% -> 0% of each run, Pallas kernels for 0% -> 0%
where the time goes in v1:
time: 94.2 us; the launch traced here: 93.4 us
  Pallas kernels  76.7 us (81%)
  local copies, waits for them, and re-layouts  10.1 us (11%)
  other arithmetic  4.06 us (4%)
  between operations  2.54 us (3%)
    pallas_call x1, Pallas kernels, on_ring(): pl.pallas_call(functools.partial(step_kernel, n), out_shape=(jax.ShapeDty...  76.7 us
    unnamed x20, local copies, waits for them, and re-layouts  4.49 us
    concatenate x2, other arithmetic, spread_halves(): jnp.concatenate([values[:, :half], pad, values[:, half:], pad], axis=1)  1.96 us

profile of v1, /device:TPU:1, one launch (start us, length us, event | category | flops | bytes accessed | tf_op | source)
XLA Modules:
  0.0 93.4 jit_solution(7436406442576962806)
XLA Ops:
  0.6 0.0 copy-start.3
  0.6 0.7 copy-done.3
  1.3 0.7 copy-done.5
  2.0 0.6 broadcast_in_dim.21.ids_row
  2.6 0.1 copy-done.2
  2.7 0.8 copy.23.kinds_col
  3.5 1.0 %fusion.3 = (f32[256,100]{0,1:T(8,128)S(1)}, f32[256,100]{0,1:T(8,128)S(1)}) fusion(f32[256,200]{0,1:T(8,128)} %param.9), kind=kLoop, calls=%fused_computation.16 | loop fusion | bytes 409600 | tf_op jit(solution)/shard_map/slice | solution.py:484
  4.5 0.1 copy.28
  4.6 0.1 copy.29
  4.7 0.0 copy-start
  4.7 0.9 pad_maximum_fusion.2.rels
  5.6 0.9 broadcast_in_dim.26.ids_col
  6.5 0.0 copy-done
  6.5 0.1 copy.26
  6.7 0.1 copy.27
  6.9 1.1 %pad_maximum_fusion.ent = f32[512,256]{1,0:T(8,128)} fusion(f32[512,28]{1,0:T(8,128)S(1)} %broadcast_in_dim.24, f32[512,100]{1,0:T(8,128)S(1)} %copy.27, f32[512,100]{1,0:T(8,128)S(1)} %copy.26), kind=kLoop, calls=%fused_computation | loop fusion | flops 393216 | bytes 991232 | tf_op jit(solution)/shard_map/concatenate | solution.py:484
  7.9 76.7 %shard_map.110 = (f32[512,256]{1,0:T(8,128)}, f32[256,256]{1,0:T(8,128)}, f32[8,128]{1,0:T(8,128)}) custom-call(s32[768,1]{1,0:T(8,128)} %broadcast_in_dim.26.ids_col, s32[1,768]{1,0:T(1,128)} %broadcast_in_dim.21.ids_row, s32[256,1]{1,0:T(8,128)} %copy.23.kinds_col, s32[1,256]{1,0:T(1,128)} %bitcast.5, f32[512,256]{1,0:T(8,128)} %pad_maximum_fusion.ent, ...), custom_call_target="tpu_custom_call" | custom-call | tf_op jit(solution)/shard_map/pallas_call | solution.py:504
  84.6 1.2 %slice.43 = f32[1,1]{1,0:T(1,128)} slice(f32[8,128]{1,0:T(8,128)} %get-tuple-element.10), slice={[0:1], [0:1]} | slice | bytes 8 | tf_op jit(solution)/shard_map/slice | solution.py:553
  86.5 1.1 %fusion = (f32[512,100]{1,0:T(8,128)S(1)}, f32[512,100]{1,0:T(8,128)S(1)}) fusion(f32[512,256]{1,0:T(8,128)} %get-tuple-element.8), kind=kLoop, calls=%fused_computation.13 | loop fusion | bytes 819200 | tf_op jit(solution)/shard_map/slice | solution.py:489
  87.5 0.0 copy-start.4
  87.6 0.3 multiply_reduce_fusion
  87.9 0.4 copy-done.4
  88.2 0.6 sqrt_add_fusion
  88.8 0.3 multiply_divide_fusion
  89.1 0.0 copy-start.1
  89.1 0.9 %copy.24 = f32[512,200]{0,1:T(8,128)} copy(f32[512,200]{1,0:T(8,128)S(1)} %multiply_divide_fusion) | data formatting | bytes 819200
  90.1 0.0 copy-start.6
  90.1 0.2 multiply_reduce_fusion.1
  90.3 0.5 copy-done.6
  90.7 0.6 sqrt_add_fusion.1
  91.3 0.2 multiply_divide_fusion.1
  91.5 0.8 copy.25
  (9 shorter events, 0.1 us)
Async XLA Ops:
  0.6 0.7 copy-start.3
  1.3 0.7 copy-start.5
  2.0 0.7 copy-start.2
  4.7 1.8 %copy-start = (f32[512,200]{0,1:T(8,128)S(1)}, f32[512,200]{0,1:T(8,128)}, u32[]{:S(2)}) copy-start(f32[512,200]{0,1:T(8,128)} %param.7) | copy-start | bytes 1228804
  87.5 0.7 copy-start.4
  89.1 1.0 %copy-start.1 = (f32[256,256]{1,0:T(8,128)S(1)}, f32[256,256]{1,0:T(8,128)}, u32[]{:S(2)}) copy-start(f32[256,256]{1,0:T(8,128)} %get-tuple-element.9) | copy-start | bytes 786436
  90.1 0.7 copy-start.6

commit v2 on v1

--- a/solution.py
+++ b/solution.py
@@ -172,7 +172,6 @@
 
 
 LANES = 128
-TAIL_ROWS = 16
 MESH = pl.DeviceIdType.MESH
 f32 = jnp.float32
 
@@ -227,25 +226,92 @@
     return loss, struck / normal, back, spread
 
 
+def lanes_of(values):
+    return lax.broadcasted_iota(jnp.int32, values.shape, 1)
+
+
+def pack_extra(extra, width):
+    count = extra.shape[0]
+    mid_lane = LANES // 2
+    narrow = width - LANES - mid_lane
+    groups = LANES // narrow
+    low, high = extra[: count // 2], extra[count // 2 :]
+    broad = jnp.where(lanes_of(low) < mid_lane, low, pltpu.roll(high, mid_lane, 1))
+    step = count // groups
+    thin = jnp.zeros((step, LANES), f32)
+    group_at = lanes_of(thin) // narrow
+    for g in range(groups):
+        moved = pltpu.roll(extra[g * step : (g + 1) * step], (g * narrow + mid_lane) % LANES, 1)
+        thin = jnp.where(group_at == g, moved, thin)
+    return broad, thin
+
+
+def unpack_extra(broad, thin, width):
+    mid_lane = LANES // 2
+    narrow = width - LANES - mid_lane
+    groups = LANES // narrow
+    from_broad = jnp.concatenate([broad, pltpu.roll(broad, mid_lane, 1)], axis=0)
+    turned = [
+        thin if (mid_lane - g * narrow) % LANES == 0 else pltpu.roll(thin, (mid_lane - g * narrow) % LANES, 1)
+        for g in range(groups)
+    ]
+    from_thin = jnp.concatenate(turned, axis=0)
+    lanes = lanes_of(from_broad)
+    return jnp.where(lanes < mid_lane, from_broad, jnp.where(lanes < width - LANES, from_thin, 0.0))
+
+
+def to_halves(natural, width):
+    half = width // 2
+    shift = LANES - half
+    base, extra = natural[:, :LANES], natural[:, LANES:]
+    lanes = lanes_of(base)
+    real = jnp.where(lanes < half, base, 0.0)
+    imag = jnp.where(lanes < shift, pltpu.roll(base, shift, 1), jnp.where(lanes < half, pltpu.roll(extra, shift, 1), 0.0))
+    return jnp.concatenate([real, imag], axis=1)
+
+
+def to_natural(halved, width):
+    half = width // 2
+    turned = pltpu.roll(halved[:, LANES:], half, 1)
+    lanes = lanes_of(turned)
+    base = jnp.where(lanes < half, halved[:, :LANES], turned)
+    return jnp.concatenate([base, jnp.where(lanes < width - LANES, turned, 0.0)], axis=1)
+
+
+def update_of(base, extra, history, width):
+    extra = jnp.where(lanes_of(extra) < width - LANES, extra, 0.0)
+    mean = jnp.sum(base * base + extra * extra, axis=1, keepdims=True) / width
+    squares = history + mean
+    scale = -learn_rate / (jnp.sqrt(squares) + adagrad_eps)
+    return base * scale, extra * scale, squares
+
+
 def step_kernel(
     n,
+    ag_sizes,
+    rs_sizes,
     ids_col,
     ids_row,
     kinds_col,
     kinds_row,
     ent,
+    ent_hist,
     rels,
-    sum_out,
+    rel_hist,
+    ent_out,
+    ent_sq_out,
     rel_out,
+    rel_sq_out,
     loss_out,
     tab,
+    wide_buf,
     rows,
     grad_hi,
     grad_lo,
     rel_local,
-    loss_local,
     pbuf,
     dbuf,
+    abuf,
     rbuf,
     fin,
     xbuf,
@@ -255,24 +321,31 @@
     ag_recv,
     pair_send,
     pair_recv,
+    cross_send,
+    cross_recv,
     rs_send,
     rs_recv,
     half_send,
     half_recv,
+    over_send,
+    over_recv,
     last_send,
     last_recv,
     rel_send,
     rel_recv,
 ):
     mid = n // 2
-    shard = ent.shape[0]
+    shard, width = ent.shape
+    rel_count = rels.shape[0]
     edges = kinds_col.shape[0]
     reads = ids_col.shape[0]
-    rel_share = rels.shape[0] // n
-    chunk = pbuf.shape[1]
+    rel_share = rel_count // n
+    packed = tab.shape[1]
+    broad_at, thin_at = shard, shard + shard // 2
     me = lax.axis_index("ea")
     lane = lax.axis_index("ba")
     core = lax.rem(lane, 2)
+    plane = lane // 2
 
     def at(place):
         place = lax.rem(place + 2 * n, n)
@@ -289,6 +362,13 @@
         pl.semaphore_signal(barrier, inc=1, device_id={"ea": lax.rem(me + j, n)}, device_id_type=MESH)
     pl.semaphore_signal(barrier, inc=1, device_id=partner, device_id_type=MESH)
     pl.semaphore_signal(barrier, inc=1, device_id=across, device_id_type=MESH)
+
+    wide_buf[...] = jnp.zeros_like(wide_buf)
+    wide_buf[:shard, : width - LANES] = ent[:, LANES:]
+    tab[0, :shard] = ent[:, :LANES]
+    broad, thin = pack_extra(wide_buf[:shard], width)
+    tab[0, broad_at:thin_at] = broad
+    tab[0, thin_at:] = thin
     pl.semaphore_wait(barrier, n + 1)
 
     sent = []
@@ -303,10 +383,13 @@
         copy.start()
         sent.append(copy)
 
-    sub = shard // 4
-
-    def ag_rows(u):
-        return pl.ds(pl.multiple_of(core * (2 * sub) + u * sub, 8), sub)
+    def span(sizes, which_core, u):
+        base, cross = sizes
+        start = which_core * (base + 2 * cross)
+        if u == 0:
+            return pl.ds(pl.multiple_of(start, 8), base)
+        chosen = plane if u == 1 else 1 - plane
+        return pl.ds(pl.multiple_of(start + base + chosen * cross, 8), cross)
 
     def ag_active(d, s, u):
         return s < mid or (s == mid and u == d)
@@ -314,48 +397,70 @@
     def ag_copy(d, s, u):
         source = (s - 1) if d == 0 else (n - (s - 1)) % n
         target = s if d == 0 else n - s
-        src = ent.at[ag_rows(u)] if s == 1 else tab.at[source, ag_rows(u)]
-        return send(src, tab.at[target, ag_rows(u)], ag_send.at[d, s - 1, u], ag_recv.at[d, s - 1, u], onward[d])
+        where = span(ag_sizes, core, u)
+        return send(tab.at[source, where], tab.at[target, where], ag_send.at[d, s - 1, u], ag_recv.at[d, s - 1, u], onward[d])
 
     def pair_copy(slot, u):
-        return send(tab.at[slot, ag_rows(u)], tab.at[slot, ag_rows(u)], pair_send.at[slot, u], pair_recv.at[slot, u], partner)
+        where = tab.at[slot, span(ag_sizes, core, u)]
+        return send(where, where, pair_send.at[slot, u], pair_recv.at[slot, u], partner)
+
+    def cross_copy(slot):
+        where = tab.at[slot, span(ag_sizes, core, 1)]
+        return send(where, where, cross_send.at[slot], cross_recv.at[slot], across)
+
+    def relay(slot):
+        cross_copy(slot).wait_recv()
+        launch(pair_copy(slot, 2))
 
     def gather(slot):
-        values = ent[...] if slot == 0 else tab[slot]
         owner = at(pos - slot)
         onehot = (ids_col[...] - owner * shard == lax.broadcasted_iota(jnp.int32, (reads, shard), 1)).astype(f32).astype(jnp.bfloat16)
-        picked = pick_rows(onehot, split_two(values))
-        if slot == 0:
+        if slot:
+            for u in range(3):
+                pair_copy(slot, u).wait_recv()
+            extra = unpack_extra(tab[slot, broad_at:thin_at], tab[slot, thin_at:], width)
+        else:
+            extra = wide_buf[:shard]
+        picked = pick_rows(onehot, split_two(jnp.concatenate([tab[slot, :shard], extra], axis=1)))
+        if slot:
+            rows[...] += picked
+        else:
             rows[...] = picked
-        else:
-            rows[...] += picked
-
-    for u in range(2):
+
+    for v in range(2):
         for d in range(2):
-            launch(ag_copy(d, 1, u if d == 0 else 1 - u))
+            launch(ag_copy(d, 1, v if d == 0 else 1 - v))
     gather(0)
-    kinds = (kinds_col[...] == lax.broadcasted_iota(jnp.int32, (edges, rels.shape[0]), 1)).astype(f32).astype(jnp.bfloat16)
-    related = pick_rows(kinds, split_two(rels[...]))
+    wide_buf[:rel_count, : width - LANES] = rels[:, LANES:]
+    kinds = (kinds_col[...] == lax.broadcasted_iota(jnp.int32, (edges, rel_count), 1)).astype(f32).astype(jnp.bfloat16)
+    related = pick_rows(kinds, split_two(jnp.concatenate([rels[:, :LANES], wide_buf[:rel_count]], axis=1)))
+    related = to_halves(related, width)
     slots_of = lambda s: (s, n - s) if s < mid else (s,)
     for s in range(1, mid + 1):
         for v in range(2):
             for d in range(2):
                 u = v if d == 0 else 1 - v
                 if ag_active(d, s, u):
+                    slot = s if d == 0 else n - s
                     ag_copy(d, s, u).wait_recv()
                     if s < mid and ag_active(d, s + 1, u):
                         launch(ag_copy(d, s + 1, u))
-                    launch(pair_copy(s if d == 0 else n - s, u))
+                    if u == 1:
+                        launch(cross_copy(slot))
+                    launch(pair_copy(slot, u))
         if s > 1:
             for slot in slots_of(s - 1):
-                for u in range(2):
-                    pair_copy(slot, u).wait_recv()
+                relay(slot)
+        if s > 2:
+            for slot in slots_of(s - 2):
                 gather(slot)
-    for u in range(2):
-        pair_copy(mid, u).wait_recv()
+    for slot in slots_of(mid - 1):
+        gather(slot)
+    relay(mid)
     gather(mid)
 
-    head, tail, contrast = rows[:edges], rows[edges : 2 * edges], rows[2 * edges :]
+    found = to_halves(rows[...], width)
+    head, tail, contrast = found[:edges], found[edges : 2 * edges], found[2 * edges :]
     query = times(head, related)
     probe = times_conj(tail, related)
     positive = jnp.sum(query * tail, axis=1, keepdims=True)
@@ -370,123 +475,157 @@
     )
     start = 0
     for part in grads:
-        upper, lower = split_two(part)
+        upper, lower = split_two(to_natural(part, width))
         grad_hi[start : start + part.shape[0]] = upper
         grad_lo[start : start + part.shape[0]] = lower
         start += part.shape[0]
-    rel_rows = times_conj(tail_back, head) + times_conj(tail, head_back)
-    kinds_t = (kinds_row[...] == lax.broadcasted_iota(jnp.int32, (rels.shape[0], edges), 0)).astype(f32).astype(jnp.bfloat16)
-    rel_local[...] = pick_rows(kinds_t, split_two(rel_rows))
-    corner = (lax.broadcasted_iota(jnp.int32, loss_local.shape, 0) == 0) & (
-        lax.broadcasted_iota(jnp.int32, loss_local.shape, 1) == 0
-    )
-    loss_local[...] = jnp.where(corner, tail_loss + head_loss, 0.0)
-
-    half = chunk // 2
-    cut = (half // 16) * 8
+
+    def sum_relations():
+        rel_rows = to_natural(times_conj(tail_back, head) + times_conj(tail, head_back), width)
+        kinds_t = (kinds_row[...] == lax.broadcasted_iota(jnp.int32, (rel_count, edges), 0)).astype(f32).astype(jnp.bfloat16)
+        shape = rel_local.shape
+        corner = (lax.rem(lax.broadcasted_iota(jnp.int32, shape, 0), rel_share) == 0) & (
+            lax.broadcasted_iota(jnp.int32, shape, 1) == shape[1] - 1
+        )
+        rel_local[...] = pick_rows(kinds_t, split_two(rel_rows)) + jnp.where(corner, tail_loss + head_loss, 0.0)
+
+    sum_relations()
+
+    half = rs_sizes[0] + 2 * rs_sizes[1]
     mine = pl.multiple_of(core * half, 8)
     other = pl.multiple_of((1 - core) * half, 8)
-    spans = ((0, cut), (cut, half - cut))
 
     def half_copy(k):
         return send(pbuf.at[k, pl.ds(other, half)], dbuf.at[k], half_send.at[k], half_recv.at[k], partner)
+
+    def over_copy(k):
+        return send(pbuf.at[k, span(rs_sizes, core, 2)], abuf.at[k], over_send.at[k], over_recv.at[k], across)
 
     def contribute(k):
         owner = at(pos + k)
         onehot = (ids_row[...] - owner * shard == lax.broadcasted_iota(jnp.int32, (shard, reads), 0)).astype(f32).astype(jnp.bfloat16)
-        pbuf[k, :shard] = pick_rows(onehot, (grad_hi[...], grad_lo[...]))
-        pbuf[k, shard : shard + rel_share] = rel_local[pl.ds(pl.multiple_of(owner * rel_share, 8), rel_share)]
-        pbuf[k, shard + rel_share :] = loss_local[...]
+        total = pick_rows(onehot, (grad_hi[...], grad_lo[...]))
+        pbuf[k, :shard] = total[:, :LANES]
+        broad, thin = pack_extra(total[:, LANES:], width)
+        pbuf[k, broad_at:thin_at] = broad
+        pbuf[k, thin_at:packed] = thin
+        share = rel_local[pl.ds(pl.multiple_of(owner * rel_share, 8), rel_share)]
+        pbuf[k, packed : packed + rel_share] = share[:, :LANES]
+        pbuf[k, packed + rel_share :] = share[:, LANES:]
         launch(half_copy(k))
+
+    def pass_over(k):
+        half_copy(k).wait_recv()
+        pbuf[k, span(rs_sizes, core, 2)] += dbuf[k, span(rs_sizes, 0, 2)]
+        launch(over_copy(k))
 
     def rs_active(d, s, u):
         return s > 1 or u == d
 
+    def ring_rows(u):
+        return pl.ds(0, rs_sizes[0]) if u == 0 else pl.ds(rs_sizes[0], rs_sizes[1])
+
     def rs_copy(d, s, u):
         k = (mid + 1 - s) if d == 0 else n - (mid + 1 - s)
-        low, size = spans[u]
         return send(
-            pbuf.at[k, pl.ds(pl.multiple_of(mine + low, 8), size)],
-            rbuf.at[d, s - 1, pl.ds(low, size)],
+            pbuf.at[k, span(rs_sizes, core, u)],
+            rbuf.at[d, s - 1, ring_rows(u)],
             rs_send.at[d, s - 1, u],
             rs_recv.at[d, s - 1, u],
             onward[d],
         )
 
-    chunks_at = lambda s: (mid,) if s == 1 else (mid + 1 - s, n - (mid + 1 - s)) if s <= mid else (0,)
-    for s in (1, 2):
+    def ring_piece(d, s, u):
+        k = (mid + 1 - s) if d == 0 else n - (mid + 1 - s)
+        total = pbuf[k, span(rs_sizes, core, u)] + dbuf[k, span(rs_sizes, 0, u)]
+        if u == 1:
+            over_copy(k).wait_recv()
+            total = total + abuf[k]
+        if s > 1 and rs_active(d, s - 1, u):
+            rs_copy(d, s - 1, u).wait_recv()
+            total = total + rbuf[d, s - 2, ring_rows(u)]
+        pbuf[k, span(rs_sizes, core, u)] = total
+        launch(rs_copy(d, s, u))
+
+    chunks_at = lambda s: (mid + 1 - s, n - (mid + 1 - s)) if s <= mid else (0,)
+    contribute(mid)
+    pass_over(mid)
+    ring_piece(0, 1, 0)
+    for k in chunks_at(2):
+        contribute(k)
+    ring_piece(1, 1, 1)
+    for s in range(2, mid + 1):
         for k in chunks_at(s):
-            contribute(k)
-    for s in range(1, mid + 1):
-        for k in chunks_at(s):
-            half_copy(k).wait_recv()
+            pass_over(k)
+        ahead = chunks_at(s + 1)
         for v in range(2):
             for d in range(2):
-                u = (1 - d) if v == 0 else d
-                if not rs_active(d, s, u):
-                    continue
-                k = (mid + 1 - s) if d == 0 else n - (mid + 1 - s)
-                low, size = spans[u]
-                here = pl.ds(pl.multiple_of(mine + low, 8), size)
-                total = pbuf[k, here] + dbuf[k, pl.ds(low, size)]
-                if s > 1 and rs_active(d, s - 1, u):
-                    rs_copy(d, s - 1, u).wait_recv()
-                    total = total + rbuf[d, s - 2, pl.ds(low, size)]
-                pbuf[k, here] = total
-                launch(rs_copy(d, s, u))
-        if s + 2 <= mid + 1:
-            for k in chunks_at(s + 2):
-                contribute(k)
-    half_copy(0).wait_recv()
-
-    def last_copy(stage, u):
-        low, size = spans[u]
+                ring_piece(d, s, (1 - d) if v == 0 else d)
+            if v < len(ahead):
+                contribute(ahead[v])
+    pass_over(0)
+
+    def last_copy(stage):
         if stage == 0:
-            return send(fin.at[pl.ds(low, size)], xbuf.at[pl.ds(low, size)], last_send.at[0, u], last_recv.at[0, u], across)
-        here = pl.ds(pl.multiple_of(mine + low, 8), size)
-        return send(full.at[here], full.at[here], last_send.at[1, u], last_recv.at[1, u], partner)
+            return send(fin, xbuf, last_send.at[0], last_recv.at[0], across)
+        if stage == 1:
+            where = full.at[span(rs_sizes, core, 1)]
+            return send(where, where, last_send.at[1], last_recv.at[1], across)
+        where = full.at[span(rs_sizes, core, stage - 2)]
+        return send(where, where, last_send.at[stage], last_recv.at[stage], partner)
 
     for u in (1, 0):
-        low, size = spans[u]
-        total = pbuf[0, pl.ds(pl.multiple_of(mine + low, 8), size)] + dbuf[0, pl.ds(low, size)]
+        total = pbuf[0, span(rs_sizes, core, u)] + dbuf[0, span(rs_sizes, 0, u)]
+        if u == 1:
+            over_copy(0).wait_recv()
+            total = total + abuf[0]
         for d in range(2):
             rs_copy(d, mid, u).wait_recv()
-            total = total + rbuf[d, mid - 1, pl.ds(low, size)]
-        fin[pl.ds(low, size)] = total
-        launch(last_copy(0, u))
-    for u in (1, 0):
-        low, size = spans[u]
-        last_copy(0, u).wait_recv()
-        full[pl.ds(pl.multiple_of(mine + low, 8), size)] = fin[pl.ds(low, size)] + xbuf[pl.ds(low, size)]
-        launch(last_copy(1, u))
-    for u in (1, 0):
-        last_copy(1, u).wait_recv()
+            total = total + rbuf[d, mid - 1, ring_rows(u)]
+        if u == 1:
+            full[span(rs_sizes, core, 1)] = total
+            launch(last_copy(1))
+            launch(last_copy(3))
+        else:
+            fin[...] = total
+            launch(last_copy(0))
+    last_copy(1).wait_recv()
+    launch(last_copy(4))
+    last_copy(0).wait_recv()
+    full[span(rs_sizes, core, 0)] = fin[...] + xbuf[...]
+    launch(last_copy(2))
+    for stage in (3, 4, 2):
+        last_copy(stage).wait_recv()
 
     def rel_copy(j):
-        return send(full.at[pl.ds(shard, rel_share)], relbuf.at[j], rel_send.at[j], rel_recv.at[j], {"ea": lax.rem(me + j, n)})
+        return send(full.at[pl.ds(packed, 2 * rel_share)], relbuf.at[j], rel_send.at[j], rel_recv.at[j], {"ea": lax.rem(me + j, n)})
 
     for j in range(1, n):
         launch(rel_copy(j))
-    sum_out[...] = full[:shard]
-    loss_out[...] = full[shard + rel_share : shard + rel_share + 8, :LANES]
-    rel_out[pl.ds(pl.multiple_of(me * rel_share, 8), rel_share)] = full[shard : shard + rel_share]
-    for j in range(1, n):
-        rel_copy(j).wait_recv()
-        source = lax.rem(me - j + n, n)
-        rel_out[pl.ds(pl.multiple_of(source * rel_share, 8), rel_share)] = relbuf[j]
+    loss_out[...] = full[packed + rel_share : packed + rel_share + 8]
+    extra = unpack_extra(full[broad_at:thin_at], full[thin_at:packed], width)
+    base_step, extra_step, squares = update_of(full[:shard], extra, ent_hist[...], width)
+    ent_out[:, :LANES] = base_step
+    ent_out[:, LANES:] = extra_step[:, : width - LANES]
+    ent_sq_out[...] = squares
+    for j in range(n):
+        if j:
+            rel_copy(j).wait_recv()
+            base, extra = relbuf[j, :rel_share], relbuf[j, rel_share:]
+        else:
+            base, extra = full[packed : packed + rel_share], full[packed + rel_share :]
+        here = pl.ds(pl.multiple_of(lax.rem(me - j + n, n) * rel_share, 8), rel_share)
+        base_step, extra_step, squares = update_of(base, extra, rel_hist[here], width)
+        rel_out[here, :LANES] = base_step
+        rel_out[here, LANES:] = extra_step[:, : width - LANES]
+        rel_sq_out[here] = squares
     for copy in sent:
         copy.wait_send()
 
 
-def spread_halves(values):
-    half = values.shape[1] // 2
-    pad = jnp.zeros((values.shape[0], LANES - half), values.dtype)
-    return jnp.concatenate([values[:, :half], pad, values[:, half:], pad], axis=1)
-
-
-def join_halves(values, width):
-    half = width // 2
-    return jnp.concatenate([values[:, :half], values[:, LANES : LANES + half]], axis=1)
+def piece_sizes(total, divisor):
+    cross = total // divisor // 8 * 8
+    return ((total - 4 * cross) // 2, cross)
 
 
 def on_ring(entities, entity_history, relations, relation_history, edge_ends, edge_relations, negatives):
@@ -496,47 +635,43 @@
     edges = edge_ends.shape[0]
     ids = jnp.concatenate([edge_ends[:, 0], edge_ends[:, 1], negatives])
     reads = ids.shape[0]
-    chunk = shard + rel_count // n + TAIL_ROWS
+    packed = shard * width // LANES
+    chunk = packed + 2 * (rel_count // n)
+    ag_sizes, rs_sizes = piece_sizes(packed, 6), piece_sizes(chunk, 7)
+    half = chunk // 2
     wide = 2 * LANES
     mid = n // 2
     dma = pltpu.SemaphoreType.DMA
     vmem = pl.BlockSpec(memory_space=pltpu.VMEM)
-    summed, rel_sum, loss = pl.pallas_call(
-        functools.partial(step_kernel, n),
+    sems = [(2, mid, 2), (n, 3), (n,), (2, mid, 2), (n,), (n,), (5,), (n,)]
+    entity_step, entity_squares, relation_step, relation_squares, loss = pl.pallas_call(
+        functools.partial(step_kernel, n, ag_sizes, rs_sizes),
         out_shape=(
-            jax.ShapeDtypeStruct((shard, wide), f32),
-            jax.ShapeDtypeStruct((rel_count, wide), f32),
+            jax.ShapeDtypeStruct((shard, width), f32),
+            jax.ShapeDtypeStruct((shard, 1), f32),
+            jax.ShapeDtypeStruct((rel_count, width), f32),
+            jax.ShapeDtypeStruct((rel_count, 1), f32),
             jax.ShapeDtypeStruct((8, LANES), f32),
         ),
-        in_specs=[vmem] * 6,
-        out_specs=(vmem,) * 3,
+        in_specs=[vmem] * 8,
+        out_specs=(vmem,) * 5,
         scratch_shapes=[
-            pltpu.VMEM((n, shard, wide), f32),
+            pltpu.VMEM((n, packed, LANES), f32),
+            pltpu.VMEM((max(shard, rel_count), LANES), f32),
             pltpu.VMEM((reads, wide), f32),
             pltpu.VMEM((reads, wide), jnp.bfloat16),
             pltpu.VMEM((reads, wide), jnp.bfloat16),
             pltpu.VMEM((rel_count, wide), f32),
-            pltpu.VMEM((TAIL_ROWS, wide), f32),
-            pltpu.VMEM((n, chunk, wide), f32),
-            pltpu.VMEM((n, chunk // 2, wide), f32),
-            pltpu.VMEM((2, mid, chunk // 2, wide), f32),
-            pltpu.VMEM((chunk // 2, wide), f32),
-            pltpu.VMEM((chunk // 2, wide), f32),
-            pltpu.VMEM((chunk, wide), f32),
-            pltpu.VMEM((n, rel_count // n, wide), f32),
-            dma((2, mid, 2)),
-            dma((2, mid, 2)),
-            dma((n, 2)),
-            dma((n, 2)),
-            dma((2, mid, 2)),
-            dma((2, mid, 2)),
-            dma((n,)),
-            dma((n,)),
-            dma((2, 2)),
-            dma((2, 2)),
-            dma((n,)),
-            dma((n,)),
-        ],
+            pltpu.VMEM((n, chunk, LANES), f32),
+            pltpu.VMEM((n, half, LANES), f32),
+            pltpu.VMEM((n, rs_sizes[1], LANES), f32),
+            pltpu.VMEM((2, mid, sum(rs_sizes), LANES), f32),
+            pltpu.VMEM((rs_sizes[0], LANES), f32),
+            pltpu.VMEM((rs_sizes[0], LANES), f32),
+            pltpu.VMEM((chunk, LANES), f32),
+            pltpu.VMEM((n, 2 * (rel_count // n), LANES), f32),
+        ]
+        + [dma(shape) for shape in sems for both in range(2)],
         compiler_params=pltpu.CompilerParams(
             collective_id=0, has_side_effects=True, vmem_limit_bytes=60 * 1024 * 1024
         ),
@@ -545,18 +680,33 @@
         ids[None, :],
         edge_relations[:, None],
         edge_relations[None, :],
-        spread_halves(entities),
-        spread_halves(relations),
-    )
-    relation_step, relation_squares = adagrad_step(join_halves(rel_sum, width), relation_history)
-    entity_step, entity_squares = adagrad_step(join_halves(summed, width), entity_history)
-    mean_loss = (loss[0, 0] / (2.0 * edges * n * lax.axis_size("ba"))).reshape(1)
-    return (entity_step, entity_squares, relation_step, relation_squares, mean_loss)
-
-
-def fits_ring(mesh):
-    n = mesh.shape["ea"]
-    return mesh.shape["ba"] == 4 and n % 2 == 0 and 4 <= n <= 16
+        entities,
+        entity_history[:, None],
+        relations,
+        relation_history[:, None],
+    )
+    mean_loss = (loss[0, LANES - 1] / (2.0 * edges * n * lax.axis_size("ba"))).reshape(1)
+    return (entity_step, entity_squares[:, 0], relation_step, relation_squares[:, 0], mean_loss)
+
+
+def fits_ring(n, n_ba, entities, relations):
+    shard, width = entities.shape
+    narrow = width - LANES - LANES // 2
+    return (
+        n_ba == 4
+        and n % 2 == 0
+        and 4 <= n <= 16
+        and width % 2 == 0
+        and 0 < narrow < LANES // 2 - 1
+        and LANES % narrow == 0
+        and shard % (8 * (LANES // narrow)) == 0
+        and relations.shape[0] % (8 * n) == 0
+    )
+
+
+def per_device(entities, entity_history, relations, relation_history, *batch):
+    fits = fits_ring(lax.axis_size("ea"), lax.axis_size("ba"), entities, relations)
+    return (on_ring if fits else on_device)(entities, entity_history, relations, relation_history, *batch)
 
 
 def solution(mesh):
@@ -570,7 +720,7 @@
         P(("ba", "ea")),
     )
     return jax.shard_map(
-        on_ring if fits_ring(mesh) else on_device,
+        per_device,
         mesh=mesh,
         in_specs=placed,
         out_specs=(P("ea", None), P("ea"), P(), P(), P()),

time: 94.2 us -> 90.3 us (0.959)
  other arithmetic: 4.06 us -> 1.41 us
  Pallas kernels: 76.7 us -> 74.8 us
  local copies, waits for them, and re-layouts: 10.1 us -> 11.3 us
    slice x5 -> x1, local copies, waits for them, and re-layouts: 3.29 us -> 1.26 us  [on_ring(): loss[0, LANES - 1] / (2.0 * edges * n * lax.axis_size('ba'))]
    concatenate x2 -> x0, other arithmetic: 1.96 us -> none  [spread_halves(): jnp.concatenate([values[:, :half], pad, values[:, half:], pad], axis=1)]
    pallas_call x1, Pallas kernels: 76.7 us -> 74.8 us  [on_ring(): pl.pallas_call(functools.partial(step_kernel, n, ag_sizes, rs_sizes), out...]
    broadcast_in_dim x2, local copies, waits for them, and re-layouts: 0.03 us -> 1.66 us  [the longest x1 0.86 us: on_ring(): entity_history[:, None]]
    unnamed x20 -> x24, local copies, waits for them, and re-layouts: 4.49 us -> 6.12 us
    pallas_call x0 -> x2, other arithmetic: none -> 1.4 us  [on_ring(): pl.pallas_call(functools.partial(step_kernel, n, ag_sizes, rs_sizes), out...]
    add x2 -> x0, other arithmetic: 1.15 us -> none  [adagrad_step(): jnp.sqrt(squares)[:, None] + adagrad_eps]
where the time goes in v2:
time: 90.3 us; the launch traced here: 90 us
  Pallas kernels  74.8 us (83%)
  local copies, waits for them, and re-layouts  11.3 us (13%)
  between operations  2.46 us (3%)
  other arithmetic  1.41 us (2%)
    pallas_call x1, Pallas kernels, on_ring(): pl.pallas_call(functools.partial(step_kernel, n, ag_sizes, rs_sizes), out...  74.8 us
    unnamed x24, local copies, waits for them, and re-layouts  6.12 us

profile of v2, /device:TPU:1, one launch (start us, length us, event | category | flops | bytes accessed | tf_op | source)
XLA Modules:
  0.0 90.0 jit_solution(17519471122599880472)
XLA Ops:
  0.6 0.0 copy-start.7
  0.6 0.7 copy-done.7
  1.3 0.0 copy-start.9
  1.3 0.7 copy-done.9
  2.0 0.0 copy-start.8
  2.0 0.6 broadcast_in_dim.19.ids_row
  2.6 0.1 copy-done.8
  2.7 0.0 copy-start.5
  2.7 0.0 copy-start.6
  2.7 0.8 copy.21.rel_hist
  3.5 0.0 copy-done.5
  3.5 0.0 copy-start.3
  3.5 0.8 copy.17.kinds_col
  4.3 0.0 copy-done.6
  4.3 0.9 copy.19.ent_hist
  5.2 0.0 copy-done.3
  5.2 0.0 copy-start
  5.2 0.8 copy.20.rels
  6.0 0.9 %broadcast_in_dim.24.ids_col = s32[768,1]{1,0:T(8,128)} reshape(s32[768]{0:T(1024)S(1)} %pad_add_fusion) | data formatting | bytes 6144 | tf_op jit(solution)/shard_map/broadcast_in_dim | solution.py:679
  6.9 0.0 copy-done
  6.9 1.0 %copy.18.ent = f32[512,200]{1,0:T(8,128)} copy(f32[512,200]{0,1:T(8,128)S(1)} %copy-done) | data formatting | bytes 819200 | tf_op args[0]
  7.9 74.8 %shard_map.110 = (f32[512,200]{1,0:T(8,128)}, f32[512,1]{1,0:T(8,128)}, f32[256,200]{1,0:T(8,128)}, f32[256,1]{1,0:T(8,128)}, f32[8,128]{1,0:T(8,128)}) custom-call(s32[768,1]{1,0:T(8,128)} %broadcast_in_dim.24.ids_col, s32[1,768]{1,0:T(1,128)} %broadcast_in_dim.19.ids_row, s32[256,1]{1,0:T(8,128)} %copy.17.kinds_col, s32[1,256]{1,0:T(1,128)} %bitcast.9, ...), custom_call_target="tpu_custom_call" | custom-call | tf_op jit(solution)/shard_map/pallas_call | solution.py:647
  82.7 1.3 %slice.11 = f32[1,1]{1,0:T(1,128)} slice(f32[8,128]{1,0:T(8,128)} %get-tuple-element.14), slice={[0:1], [127:128]} | slice | bytes 8 | tf_op jit(solution)/shard_map/slice | solution.py:688
  84.6 0.0 copy-start.4
  84.6 0.0 copy-start.2
  84.6 2.0 %copy.22 = f32[512,200]{0,1:T(8,128)} copy(f32[512,200]{1,0:T(8,128)} %get-tuple-element.20) | data formatting | bytes 819200
  86.7 0.0 copy-done.4
  86.7 0.7 reduce.1
  87.4 0.0 copy-done.2
  87.4 0.7 reduce
  88.1 0.0 copy-done.1
  88.1 0.8 copy.23
  (3 shorter events, 0.0 us)
Async XLA Ops:
  0.6 0.7 copy-start.7
  1.3 0.7 copy-start.9
  2.0 0.7 copy-start.8
  2.7 0.8 copy-start.5
  2.7 1.6 %copy-start.6 = (f32[512]{0:T(512)S(1)}, f32[512]{0:T(512)}, u32[]{:S(2)}) copy-start(f32[512]{0:T(512)} %param.8) | copy-start | bytes 6148
  3.5 1.7 %copy-start.3 = (f32[256,200]{0,1:T(8,128)S(1)}, f32[256,200]{0,1:T(8,128)}, u32[]{:S(2)}) copy-start(f32[256,200]{0,1:T(8,128)} %param.9) | copy-start | bytes 614404
  5.2 1.7 %copy-start = (f32[512,200]{0,1:T(8,128)S(1)}, f32[512,200]{0,1:T(8,128)}, u32[]{:S(2)}) copy-start(f32[512,200]{0,1:T(8,128)} %param.7) | copy-start | bytes 1228804
  84.6 2.1 %copy-start.4 = (f32[256,1]{1,0:T(8,128)S(1)}, f32[256,1]{1,0:T(8,128)}, u32[]{:S(2)}) copy-start(f32[256,1]{1,0:T(8,128)} %get-tuple-element.13) | copy-start | bytes 3076
  84.6 2.7 %copy-start.2 = (f32[512,1]{1,0:T(8,128)S(1)}, f32[512,1]{1,0:T(8,128)}, u32[]{:S(2)}) copy-start(f32[512,1]{1,0:T(8,128)} %get-tuple-element.11) | copy-start | bytes 6148
  86.7 1.4 %copy-start.1 = (f32[256,200]{1,0:T(8,128)S(1)}, f32[256,200]{1,0:T(8,128)}, u32[]{:S(2)}) copy-start(f32[256,200]{1,0:T(8,128)} %get-tuple-element.22) | copy-start | bytes 614404

commit v3 on v2

--- a/solution.py
+++ b/solution.py
@@ -226,73 +226,38 @@
     return loss, struck / normal, back, spread
 
 
-def lanes_of(values):
-    return lax.broadcasted_iota(jnp.int32, values.shape, 1)
-
-
-def pack_extra(extra, width):
-    count = extra.shape[0]
-    mid_lane = LANES // 2
-    narrow = width - LANES - mid_lane
-    groups = LANES // narrow
-    low, high = extra[: count // 2], extra[count // 2 :]
-    broad = jnp.where(lanes_of(low) < mid_lane, low, pltpu.roll(high, mid_lane, 1))
-    step = count // groups
-    thin = jnp.zeros((step, LANES), f32)
-    group_at = lanes_of(thin) // narrow
-    for g in range(groups):
-        moved = pltpu.roll(extra[g * step : (g + 1) * step], (g * narrow + mid_lane) % LANES, 1)
-        thin = jnp.where(group_at == g, moved, thin)
-    return broad, thin
-
-
-def unpack_extra(broad, thin, width):
-    mid_lane = LANES // 2
-    narrow = width - LANES - mid_lane
-    groups = LANES // narrow
-    from_broad = jnp.concatenate([broad, pltpu.roll(broad, mid_lane, 1)], axis=0)
-    turned = [
-        thin if (mid_lane - g * narrow) % LANES == 0 else pltpu.roll(thin, (mid_lane - g * narrow) % LANES, 1)
-        for g in range(groups)
-    ]
-    from_thin = jnp.concatenate(turned, axis=0)
-    lanes = lanes_of(from_broad)
-    return jnp.where(lanes < mid_lane, from_broad, jnp.where(lanes < width - LANES, from_thin, 0.0))
-
-
-def to_halves(natural, width):
+def to_halves(turned, width):
     half = width // 2
-    shift = LANES - half
-    base, extra = natural[:, :LANES], natural[:, LANES:]
-    lanes = lanes_of(base)
-    real = jnp.where(lanes < half, base, 0.0)
-    imag = jnp.where(lanes < shift, pltpu.roll(base, shift, 1), jnp.where(lanes < half, pltpu.roll(extra, shift, 1), 0.0))
-    return jnp.concatenate([real, imag], axis=1)
-
-
-def to_natural(halved, width):
+    pad = jnp.zeros((LANES - half, turned.shape[1]), f32)
+    return jnp.concatenate([turned[:half], pad, turned[half:width], pad], axis=0).T
+
+
+def to_turned(halved, width):
     half = width // 2
-    turned = pltpu.roll(halved[:, LANES:], half, 1)
-    lanes = lanes_of(turned)
-    base = jnp.where(lanes < half, halved[:, :LANES], turned)
-    return jnp.concatenate([base, jnp.where(lanes < width - LANES, turned, 0.0)], axis=1)
-
-
-def update_of(base, extra, history, width):
-    extra = jnp.where(lanes_of(extra) < width - LANES, extra, 0.0)
-    mean = jnp.sum(base * base + extra * extra, axis=1, keepdims=True) / width
-    squares = history + mean
-    scale = -learn_rate / (jnp.sqrt(squares) + adagrad_eps)
-    return base * scale, extra * scale, squares
+    turned = halved.T
+    return jnp.concatenate([turned[:half], turned[LANES : LANES + half]], axis=0)
+
+
+def place_rows(turned, onehot):
+    dims = ((1,), (1,))
+    return dot_of(turned[0], onehot, dims) + dot_of(turned[1], onehot, dims)
+
+
+def pick_turned(turned, onehot):
+    dims = ((1,), (0,))
+    return dot_of(turned[0], onehot, dims) + dot_of(turned[1], onehot, dims)
+
+
+def update_of(total, history):
+    squares = history + jnp.sum(total * total, axis=0, keepdims=True) / total.shape[0]
+    return total * (-learn_rate / (jnp.sqrt(squares) + adagrad_eps)), squares
 
 
 def step_kernel(
     n,
     ag_sizes,
     rs_sizes,
-    ids_col,
     ids_row,
-    kinds_col,
     kinds_row,
     ent,
     ent_hist,
@@ -304,7 +269,6 @@
     rel_sq_out,
     loss_out,
     tab,
-    wide_buf,
     rows,
     grad_hi,
     grad_lo,
@@ -317,6 +281,7 @@
     xbuf,
     full,
     relbuf,
+    rel_sum,
     ag_send,
     ag_recv,
     pair_send,
@@ -335,13 +300,13 @@
     rel_recv,
 ):
     mid = n // 2
-    shard, width = ent.shape
-    rel_count = rels.shape[0]
-    edges = kinds_col.shape[0]
-    reads = ids_col.shape[0]
-    rel_share = rel_count // n
-    packed = tab.shape[1]
-    broad_at, thin_at = shard, shard + shard // 2
+    width, shard = ent.shape
+    rel_count = rels.shape[1]
+    edges = kinds_row.shape[1]
+    reads = ids_row.shape[1]
+    rel_pad = rel_local.shape[0]
+    rel_share = rel_pad // n
+    side = shard // 2
     me = lax.axis_index("ea")
     lane = lax.axis_index("ba")
     core = lax.rem(lane, 2)
@@ -363,12 +328,6 @@
     pl.semaphore_signal(barrier, inc=1, device_id=partner, device_id_type=MESH)
     pl.semaphore_signal(barrier, inc=1, device_id=across, device_id_type=MESH)
 
-    wide_buf[...] = jnp.zeros_like(wide_buf)
-    wide_buf[:shard, : width - LANES] = ent[:, LANES:]
-    tab[0, :shard] = ent[:, :LANES]
-    broad, thin = pack_extra(wide_buf[:shard], width)
-    tab[0, broad_at:thin_at] = broad
-    tab[0, thin_at:] = thin
     pl.semaphore_wait(barrier, n + 1)
 
     sent = []
@@ -385,11 +344,11 @@
 
     def span(sizes, which_core, u):
         base, cross = sizes
-        start = which_core * (base + 2 * cross)
+        across_lanes = pl.ds(0, side) if which_core is None else pl.ds(pl.multiple_of(which_core * side, LANES), side)
         if u == 0:
-            return pl.ds(pl.multiple_of(start, 8), base)
+            return pl.ds(0, base), across_lanes
         chosen = plane if u == 1 else 1 - plane
-        return pl.ds(pl.multiple_of(start + base + chosen * cross, 8), cross)
+        return pl.ds(pl.multiple_of(base + chosen * cross, 8), cross), across_lanes
 
     def ag_active(d, s, u):
         return s < mid or (s == mid and u == d)
@@ -398,30 +357,32 @@
         source = (s - 1) if d == 0 else (n - (s - 1)) % n
         target = s if d == 0 else n - s
         where = span(ag_sizes, core, u)
-        return send(tab.at[source, where], tab.at[target, where], ag_send.at[d, s - 1, u], ag_recv.at[d, s - 1, u], onward[d])
+        src = ent.at[where] if s == 1 else tab.at[(source, *where)]
+        return send(src, tab.at[(target, *where)], ag_send.at[d, s - 1, u], ag_recv.at[d, s - 1, u], onward[d])
 
     def pair_copy(slot, u):
-        where = tab.at[slot, span(ag_sizes, core, u)]
+        where = tab.at[(slot, *span(ag_sizes, core, u))]
         return send(where, where, pair_send.at[slot, u], pair_recv.at[slot, u], partner)
 
     def cross_copy(slot):
-        where = tab.at[slot, span(ag_sizes, core, 1)]
+        where = tab.at[(slot, *span(ag_sizes, core, 1))]
         return send(where, where, cross_send.at[slot], cross_recv.at[slot], across)
 
     def relay(slot):
         cross_copy(slot).wait_recv()
         launch(pair_copy(slot, 2))
 
+    def onehot_of(owner):
+        places = lax.broadcasted_iota(jnp.int32, (shard, reads), 0)
+        return (ids_row[...] - owner * shard == places).astype(f32).astype(jnp.bfloat16)
+
     def gather(slot):
         owner = at(pos - slot)
-        onehot = (ids_col[...] - owner * shard == lax.broadcasted_iota(jnp.int32, (reads, shard), 1)).astype(f32).astype(jnp.bfloat16)
+        onehot = onehot_of(owner)
         if slot:
             for u in range(3):
                 pair_copy(slot, u).wait_recv()
-            extra = unpack_extra(tab[slot, broad_at:thin_at], tab[slot, thin_at:], width)
-        else:
-            extra = wide_buf[:shard]
-        picked = pick_rows(onehot, split_two(jnp.concatenate([tab[slot, :shard], extra], axis=1)))
+        picked = pick_turned(split_two(tab[slot] if slot else ent[...]), onehot)
         if slot:
             rows[...] += picked
         else:
@@ -431,10 +392,8 @@
         for d in range(2):
             launch(ag_copy(d, 1, v if d == 0 else 1 - v))
     gather(0)
-    wide_buf[:rel_count, : width - LANES] = rels[:, LANES:]
-    kinds = (kinds_col[...] == lax.broadcasted_iota(jnp.int32, (edges, rel_count), 1)).astype(f32).astype(jnp.bfloat16)
-    related = pick_rows(kinds, split_two(jnp.concatenate([rels[:, :LANES], wide_buf[:rel_count]], axis=1)))
-    related = to_halves(related, width)
+    kinds = (kinds_row[...] == lax.broadcasted_iota(jnp.int32, (rel_count, edges), 0)).astype(f32).astype(jnp.bfloat16)
+    related = to_halves(pick_turned(split_two(rels[...]), kinds), width)
     slots_of = lambda s: (s, n - s) if s < mid else (s,)
     for s in range(1, mid + 1):
         for v in range(2):
@@ -475,48 +434,36 @@
     )
     start = 0
     for part in grads:
-        upper, lower = split_two(to_natural(part, width))
-        grad_hi[start : start + part.shape[0]] = upper
-        grad_lo[start : start + part.shape[0]] = lower
+        upper, lower = split_two(to_turned(part, width))
+        grad_hi[:, start : start + part.shape[0]] = upper
+        grad_lo[:, start : start + part.shape[0]] = lower
         start += part.shape[0]
-
-    def sum_relations():
-        rel_rows = to_natural(times_conj(tail_back, head) + times_conj(tail, head_back), width)
-        kinds_t = (kinds_row[...] == lax.broadcasted_iota(jnp.int32, (rel_count, edges), 0)).astype(f32).astype(jnp.bfloat16)
-        shape = rel_local.shape
-        corner = (lax.rem(lax.broadcasted_iota(jnp.int32, shape, 0), rel_share) == 0) & (
-            lax.broadcasted_iota(jnp.int32, shape, 1) == shape[1] - 1
-        )
-        rel_local[...] = pick_rows(kinds_t, split_two(rel_rows)) + jnp.where(corner, tail_loss + head_loss, 0.0)
-
-    sum_relations()
-
-    half = rs_sizes[0] + 2 * rs_sizes[1]
-    mine = pl.multiple_of(core * half, 8)
-    other = pl.multiple_of((1 - core) * half, 8)
+    rel_rows = to_turned(times_conj(tail_back, head) + times_conj(tail, head_back), width)
+    rel_local[:width] = place_rows(split_two(rel_rows), kinds)
+    corner = (rel_pad - width, rel_count)
+    first = lax.broadcasted_iota(jnp.int32, corner, 0) + lax.broadcasted_iota(jnp.int32, corner, 1) == 0
+    rel_local[width:] = jnp.where(first, tail_loss + head_loss, 0.0)
+
+    other = pl.ds(pl.multiple_of((1 - core) * side, LANES), side)
 
     def half_copy(k):
-        return send(pbuf.at[k, pl.ds(other, half)], dbuf.at[k], half_send.at[k], half_recv.at[k], partner)
+        return send(pbuf.at[k, :, other], dbuf.at[k], half_send.at[k], half_recv.at[k], partner)
 
     def over_copy(k):
-        return send(pbuf.at[k, span(rs_sizes, core, 2)], abuf.at[k], over_send.at[k], over_recv.at[k], across)
+        return send(pbuf.at[(k, *span(rs_sizes, core, 2))], abuf.at[k], over_send.at[k], over_recv.at[k], across)
 
     def contribute(k):
         owner = at(pos + k)
-        onehot = (ids_row[...] - owner * shard == lax.broadcasted_iota(jnp.int32, (shard, reads), 0)).astype(f32).astype(jnp.bfloat16)
-        total = pick_rows(onehot, (grad_hi[...], grad_lo[...]))
-        pbuf[k, :shard] = total[:, :LANES]
-        broad, thin = pack_extra(total[:, LANES:], width)
-        pbuf[k, broad_at:thin_at] = broad
-        pbuf[k, thin_at:packed] = thin
-        share = rel_local[pl.ds(pl.multiple_of(owner * rel_share, 8), rel_share)]
-        pbuf[k, packed : packed + rel_share] = share[:, :LANES]
-        pbuf[k, packed + rel_share :] = share[:, LANES:]
+        pbuf[k, :width] = place_rows((grad_hi[...], grad_lo[...]), onehot_of(owner))
+        low = pl.multiple_of(owner * rel_share, 8)
+        for part in range(2):
+            share = rel_local[pl.ds(pl.multiple_of(low + part * (rel_share // 2), 8), rel_share // 2)]
+            pbuf[k, width:, part * rel_count : (part + 1) * rel_count] = share
         launch(half_copy(k))
 
     def pass_over(k):
         half_copy(k).wait_recv()
-        pbuf[k, span(rs_sizes, core, 2)] += dbuf[k, span(rs_sizes, 0, 2)]
+        pbuf[(k, *span(rs_sizes, core, 2))] = pbuf[(k, *span(rs_sizes, core, 2))] + dbuf[(k, *span(rs_sizes, None, 2))]
         launch(over_copy(k))
 
     def rs_active(d, s, u):
@@ -528,7 +475,7 @@
     def rs_copy(d, s, u):
         k = (mid + 1 - s) if d == 0 else n - (mid + 1 - s)
         return send(
-            pbuf.at[k, span(rs_sizes, core, u)],
+            pbuf.at[(k, *span(rs_sizes, core, u))],
             rbuf.at[d, s - 1, ring_rows(u)],
             rs_send.at[d, s - 1, u],
             rs_recv.at[d, s - 1, u],
@@ -537,14 +484,14 @@
 
     def ring_piece(d, s, u):
         k = (mid + 1 - s) if d == 0 else n - (mid + 1 - s)
-        total = pbuf[k, span(rs_sizes, core, u)] + dbuf[k, span(rs_sizes, 0, u)]
+        total = pbuf[(k, *span(rs_sizes, core, u))] + dbuf[(k, *span(rs_sizes, None, u))]
         if u == 1:
             over_copy(k).wait_recv()
             total = total + abuf[k]
         if s > 1 and rs_active(d, s - 1, u):
             rs_copy(d, s - 1, u).wait_recv()
             total = total + rbuf[d, s - 2, ring_rows(u)]
-        pbuf[k, span(rs_sizes, core, u)] = total
+        pbuf[(k, *span(rs_sizes, core, u))] = total
         launch(rs_copy(d, s, u))
 
     chunks_at = lambda s: (mid + 1 - s, n - (mid + 1 - s)) if s <= mid else (0,)
@@ -575,7 +522,7 @@
         return send(where, where, last_send.at[stage], last_recv.at[stage], partner)
 
     for u in (1, 0):
-        total = pbuf[0, span(rs_sizes, core, u)] + dbuf[0, span(rs_sizes, 0, u)]
+        total = pbuf[(0, *span(rs_sizes, core, u))] + dbuf[(0, *span(rs_sizes, None, u))]
         if u == 1:
             over_copy(0).wait_recv()
             total = total + abuf[0]
@@ -598,34 +545,28 @@
         last_copy(stage).wait_recv()
 
     def rel_copy(j):
-        return send(full.at[pl.ds(packed, 2 * rel_share)], relbuf.at[j], rel_send.at[j], rel_recv.at[j], {"ea": lax.rem(me + j, n)})
+        return send(full.at[pl.ds(width, rel_share // 2)], relbuf.at[j], rel_send.at[j], rel_recv.at[j], {"ea": lax.rem(me + j, n)})
 
     for j in range(1, n):
         launch(rel_copy(j))
-    loss_out[...] = full[packed + rel_share : packed + rel_share + 8]
-    extra = unpack_extra(full[broad_at:thin_at], full[thin_at:packed], width)
-    base_step, extra_step, squares = update_of(full[:shard], extra, ent_hist[...], width)
-    ent_out[:, :LANES] = base_step
-    ent_out[:, LANES:] = extra_step[:, : width - LANES]
-    ent_sq_out[...] = squares
+    ent_out[...], ent_sq_out[...] = update_of(full[:width], ent_hist[...])
     for j in range(n):
         if j:
             rel_copy(j).wait_recv()
-            base, extra = relbuf[j, :rel_share], relbuf[j, rel_share:]
-        else:
-            base, extra = full[packed : packed + rel_share], full[packed + rel_share :]
-        here = pl.ds(pl.multiple_of(lax.rem(me - j + n, n) * rel_share, 8), rel_share)
-        base_step, extra_step, squares = update_of(base, extra, rel_hist[here], width)
-        rel_out[here, :LANES] = base_step
-        rel_out[here, LANES:] = extra_step[:, : width - LANES]
-        rel_sq_out[here] = squares
+        low = pl.multiple_of(lax.rem(me - j + n, n) * rel_share, 8)
+        for part in range(2):
+            columns = pl.ds(part * rel_count, rel_count)
+            share = relbuf[j, :, columns] if j else full[pl.ds(width, rel_share // 2), columns]
+            rel_sum[pl.ds(pl.multiple_of(low + part * (rel_share // 2), 8), rel_share // 2)] = share
+    rel_out[...], rel_sq_out[...] = update_of(rel_sum[:width], rel_hist[...])
+    loss_out[...] = rel_sum[width : width + 8, :LANES]
     for copy in sent:
         copy.wait_send()
 
 
 def piece_sizes(total, divisor):
     cross = total // divisor // 8 * 8
-    return ((total - 4 * cross) // 2, cross)
+    return (total - 2 * cross, cross)
 
 
 def on_ring(entities, entity_history, relations, relation_history, edge_ends, edge_relations, negatives):
@@ -635,11 +576,10 @@
     edges = edge_ends.shape[0]
     ids = jnp.concatenate([edge_ends[:, 0], edge_ends[:, 1], negatives])
     reads = ids.shape[0]
-    packed = shard * width // LANES
-    chunk = packed + 2 * (rel_count // n)
-    ag_sizes, rs_sizes = piece_sizes(packed, 6), piece_sizes(chunk, 7)
-    half = chunk // 2
-    wide = 2 * LANES
+    rel_pad = -(-(width + 8) // (16 * n)) * 16 * n
+    chunk = width + rel_pad // n // 2
+    ag_sizes, rs_sizes = piece_sizes(width, 3), piece_sizes(chunk, 3)
+    side = shard // 2
     mid = n // 2
     dma = pltpu.SemaphoreType.DMA
     vmem = pl.BlockSpec(memory_space=pltpu.VMEM)
@@ -647,60 +587,56 @@
     entity_step, entity_squares, relation_step, relation_squares, loss = pl.pallas_call(
         functools.partial(step_kernel, n, ag_sizes, rs_sizes),
         out_shape=(
-            jax.ShapeDtypeStruct((shard, width), f32),
-            jax.ShapeDtypeStruct((shard, 1), f32),
-            jax.ShapeDtypeStruct((rel_count, width), f32),
-            jax.ShapeDtypeStruct((rel_count, 1), f32),
+            jax.ShapeDtypeStruct((width, shard), f32),
+            jax.ShapeDtypeStruct((1, shard), f32),
+            jax.ShapeDtypeStruct((width, rel_count), f32),
+            jax.ShapeDtypeStruct((1, rel_count), f32),
             jax.ShapeDtypeStruct((8, LANES), f32),
         ),
-        in_specs=[vmem] * 8,
+        in_specs=[vmem] * 6,
         out_specs=(vmem,) * 5,
         scratch_shapes=[
-            pltpu.VMEM((n, packed, LANES), f32),
-            pltpu.VMEM((max(shard, rel_count), LANES), f32),
-            pltpu.VMEM((reads, wide), f32),
-            pltpu.VMEM((reads, wide), jnp.bfloat16),
-            pltpu.VMEM((reads, wide), jnp.bfloat16),
-            pltpu.VMEM((rel_count, wide), f32),
-            pltpu.VMEM((n, chunk, LANES), f32),
-            pltpu.VMEM((n, half, LANES), f32),
-            pltpu.VMEM((n, rs_sizes[1], LANES), f32),
-            pltpu.VMEM((2, mid, sum(rs_sizes), LANES), f32),
-            pltpu.VMEM((rs_sizes[0], LANES), f32),
-            pltpu.VMEM((rs_sizes[0], LANES), f32),
-            pltpu.VMEM((chunk, LANES), f32),
-            pltpu.VMEM((n, 2 * (rel_count // n), LANES), f32),
+            pltpu.VMEM((n, width, shard), f32),
+            pltpu.VMEM((width, reads), f32),
+            pltpu.VMEM((width, reads), jnp.bfloat16),
+            pltpu.VMEM((width, reads), jnp.bfloat16),
+            pltpu.VMEM((rel_pad, rel_count), f32),
+            pltpu.VMEM((n, chunk, shard), f32),
+            pltpu.VMEM((n, chunk, side), f32),
+            pltpu.VMEM((n, rs_sizes[1], side), f32),
+            pltpu.VMEM((2, mid, sum(rs_sizes), side), f32),
+            pltpu.VMEM((rs_sizes[0], side), f32),
+            pltpu.VMEM((rs_sizes[0], side), f32),
+            pltpu.VMEM((chunk, shard), f32),
+            pltpu.VMEM((n, rel_pad // n // 2, shard), f32),
+            pltpu.VMEM((rel_pad, rel_count), f32),
         ]
         + [dma(shape) for shape in sems for both in range(2)],
         compiler_params=pltpu.CompilerParams(
             collective_id=0, has_side_effects=True, vmem_limit_bytes=60 * 1024 * 1024
         ),
     )(
-        ids[:, None],
         ids[None, :],
-        edge_relations[:, None],
         edge_relations[None, :],
-        entities,
-        entity_history[:, None],
-        relations,
-        relation_history[:, None],
-    )
-    mean_loss = (loss[0, LANES - 1] / (2.0 * edges * n * lax.axis_size("ba"))).reshape(1)
-    return (entity_step, entity_squares[:, 0], relation_step, relation_squares[:, 0], mean_loss)
+        entities.T,
+        entity_history[None, :],
+        relations.T,
+        relation_history[None, :],
+    )
+    mean_loss = (loss[0, 0] / (2.0 * edges * n * lax.axis_size("ba"))).reshape(1)
+    return (entity_step.T, entity_squares[0], relation_step.T, relation_squares[0], mean_loss)
 
 
 def fits_ring(n, n_ba, entities, relations):
     shard, width = entities.shape
-    narrow = width - LANES - LANES // 2
     return (
         n_ba == 4
         and n % 2 == 0
         and 4 <= n <= 16
-        and width % 2 == 0
-        and 0 < narrow < LANES // 2 - 1
-        and LANES % narrow == 0
-        and shard % (8 * (LANES // narrow)) == 0
-        and relations.shape[0] % (8 * n) == 0
+        and width % 8 == 0
+        and width <= 2 * LANES
+        and shard % (2 * LANES) == 0
+        and 2 * relations.shape[0] == shard
     )
 
 

time: 90.3 us -> 80.6 us (0.89)
  local copies, waits for them, and re-layouts: 11.3 us -> 6.79 us
  Pallas kernels: 74.8 us -> 71.1 us
  other arithmetic: 1.41 us -> 0.01 us
    pallas_call x1, Pallas kernels: 74.8 us -> 71.1 us  [on_ring(): pl.pallas_call(functools.partial(step_kernel, n, ag_sizes, rs_sizes), out...]
    broadcast_in_dim x4 -> x0, local copies, waits for them, and re-layouts: 3.37 us -> none  [the longest x1 0.91 us: on_ring(): ids[:, None]]
    pallas_call x2 -> x0, other arithmetic: 1.4 us -> none  [on_ring(): pl.pallas_call(functools.partial(step_kernel, n, ag_sizes, rs_sizes), out...]
    unnamed x24 -> x14, local copies, waits for them, and re-layouts: 6.12 us -> 5.01 us
where the time goes in v3:
time: 80.6 us; the launch traced here: 80.4 us
  Pallas kernels  71.1 us (88%)
  local copies, waits for them, and re-layouts  6.79 us (8%)
  between operations  2.45 us (3%)
    pallas_call x1, Pallas kernels, on_ring(): pl.pallas_call(functools.partial(step_kernel, n, ag_sizes, rs_sizes), out...  71.1 us
    unnamed x14, local copies, waits for them, and re-layouts  5.01 us

profile of v3, /device:TPU:1, one launch (start us, length us, event | category | flops | bytes accessed | tf_op | source)
XLA Modules:
  0.0 80.4 jit_solution(2230215464424257192)
XLA Ops:
  0.6 0.0 copy-start.1
  0.6 0.7 copy-done.1
  1.3 0.0 copy-start.3
  1.3 0.7 copy-done.3
  2.0 0.6 broadcast_in_dim.12.ids_row
  2.6 71.1 %shard_map.110 = (f32[200,512]{1,0:T(8,128)}, f32[1,512]{1,0:T(1,128)}, f32[200,256]{1,0:T(8,128)}, f32[1,256]{1,0:T(1,128)}, f32[8,128]{1,0:T(8,128)}) custom-call(s32[1,768]{1,0:T(1,128)} %broadcast_in_dim.12.ids_row, s32[1,256]{1,0:T(1,128)} %bitcast.20, f32[200,512]{1,0:T(8,128)} %bitcast.12, f32[1,512]{1,0:T(1,128)} %bitcast.18, f32[200,256]{1,0:T(8,128)} %bitcast.14, ...), custom_call_target="tpu_custom_call" | custom-call | tf_op jit(solution)/shard_map/pallas_call | solution.py:587
  73.7 1.2 %slice.11 = f32[1,1]{1,0:T(1,128)} slice(f32[8,128]{1,0:T(8,128)} %get-tuple-element.14), slice={[0:1], [0:1]} | slice | bytes 8 | tf_op jit(solution)/shard_map/slice | solution.py:626
  75.6 0.0 copy-start.2
  75.6 0.0 copy-start
  75.6 1.8 %copy.16 = f32[512,200]{0,1:T(8,128)} copy(f32[512,200]{0,1:T(8,128)} %bitcast.13) | data formatting | bytes 819200
  77.4 0.0 copy-done.2
  77.4 0.6 copy.17
  78.0 0.0 copy-done
  78.0 0.0 copy-start.4
  78.0 0.7 copy.18
  78.7 0.0 copy-done.4
  78.7 0.6 copy.19
  (2 shorter events, 0.0 us)
Async XLA Ops:
  0.6 0.7 copy-start.1
  1.3 0.7 copy-start.3
  75.6 1.8 %copy-start.2 = (f32[1,512]{1,0:T(1,128)S(1)}, f32[1,512]{1,0:T(1,128)}, u32[]{:S(2)}) copy-start(f32[1,512]{1,0:T(1,128)} %get-tuple-element.11) | copy-start | bytes 6148
  75.6 2.4 %copy-start = (f32[200,256]{1,0:T(8,128)S(1)}, f32[200,256]{1,0:T(8,128)}, u32[]{:S(2)}) copy-start(f32[200,256]{1,0:T(8,128)} %get-tuple-element.12) | copy-start | bytes 614404
  78.0 0.7 copy-start.4

commit v4 on v3

--- a/solution.py
+++ b/solution.py
@@ -538,17 +538,19 @@
             launch(last_copy(0))
     last_copy(1).wait_recv()
     launch(last_copy(4))
+    for stage in (3, 4):
+        last_copy(stage).wait_recv()
+
+    def rel_copy(j):
+        return send(full.at[pl.ds(width, rel_share // 2)], relbuf.at[j], rel_send.at[j], rel_recv.at[j], {"ea": lax.rem(me + j, n)})
+
+    for j in range(1, n):
+        launch(rel_copy(j))
     last_copy(0).wait_recv()
     full[span(rs_sizes, core, 0)] = fin[...] + xbuf[...]
     launch(last_copy(2))
-    for stage in (3, 4, 2):
-        last_copy(stage).wait_recv()
-
-    def rel_copy(j):
-        return send(full.at[pl.ds(width, rel_share // 2)], relbuf.at[j], rel_send.at[j], rel_recv.at[j], {"ea": lax.rem(me + j, n)})
-
-    for j in range(1, n):
-        launch(rel_copy(j))
+    last_copy(2).wait_recv()
+
     ent_out[...], ent_sq_out[...] = update_of(full[:width], ent_hist[...])
     for j in range(n):
         if j:
@@ -559,7 +561,7 @@
             share = relbuf[j, :, columns] if j else full[pl.ds(width, rel_share // 2), columns]
             rel_sum[pl.ds(pl.multiple_of(low + part * (rel_share // 2), 8), rel_share // 2)] = share
     rel_out[...], rel_sq_out[...] = update_of(rel_sum[:width], rel_hist[...])
-    loss_out[...] = rel_sum[width : width + 8, :LANES]
+    loss_out[...] = rel_sum[width : width + 1, :1] / (2.0 * edges * n * 4)
     for copy in sent:
         copy.wait_send()
 
@@ -591,7 +593,7 @@
             jax.ShapeDtypeStruct((1, shard), f32),
             jax.ShapeDtypeStruct((width, rel_count), f32),
             jax.ShapeDtypeStruct((1, rel_count), f32),
-            jax.ShapeDtypeStruct((8, LANES), f32),
+            jax.ShapeDtypeStruct((1, 1), f32),
         ),
         in_specs=[vmem] * 6,
         out_specs=(vmem,) * 5,
@@ -623,7 +625,7 @@
         relations.T,
         relation_history[None, :],
     )
-    mean_loss = (loss[0, 0] / (2.0 * edges * n * lax.axis_size("ba"))).reshape(1)
+    mean_loss = loss.reshape(1)
     return (entity_step.T, entity_squares[0], relation_step.T, relation_squares[0], mean_loss)
 
 
@@ -637,6 +639,7 @@
         and width <= 2 * LANES
         and shard % (2 * LANES) == 0
         and 2 * relations.shape[0] == shard
+        and 3 * (width // 8) > 2 * n
     )
 
 

time: 80.6 us -> 78 us (0.968)
  Pallas kernels: 71.1 us -> 69.8 us
  local copies, waits for them, and re-layouts: 6.79 us -> 5.59 us
    pallas_call x1, Pallas kernels: 71.1 us -> 69.8 us  [on_ring(): pl.pallas_call(functools.partial(step_kernel, n, ag_sizes, rs_sizes), out...]
    slice x1 -> x0, local copies, waits for them, and re-layouts: 1.2 us -> none  [on_ring(): loss[0, 0] / (2.0 * edges * n * lax.axis_size('ba'))]
where the time goes in v4:
time: 78 us; the launch traced here: 77.7 us
  Pallas kernels  69.8 us (89%)
  local copies, waits for them, and re-layouts  5.59 us (7%)
  between operations  2.35 us (3%)
    pallas_call x1, Pallas kernels, on_ring(): pl.pallas_call(functools.partial(step_kernel, n, ag_sizes, rs_sizes), out...  69.8 us
    unnamed x14, local copies, waits for them, and re-layouts  5.01 us

profile of v4, /device:TPU:1, one launch (start us, length us, event | category | flops | bytes accessed | tf_op | source)
XLA Modules:
  0.0 77.7 jit_solution(2627140486966103569)
XLA Ops:
  0.6 0.0 copy-start.1
  0.6 0.7 copy-done.1
  1.3 0.0 copy-start.3
  1.3 0.7 copy-done.3
  2.0 0.6 broadcast_in_dim.12.ids_row
  2.6 69.8 %shard_map.110 = (f32[200,512]{1,0:T(8,128)}, f32[1,512]{1,0:T(1,128)}, f32[200,256]{1,0:T(8,128)}, f32[1,256]{1,0:T(1,128)}, f32[1,1]{1,0:T(1,128)}) custom-call(s32[1,768]{1,0:T(1,128)} %broadcast_in_dim.12.ids_row, s32[1,256]{1,0:T(1,128)} %bitcast.20, f32[200,512]{1,0:T(8,128)} %bitcast.12, f32[1,512]{1,0:T(1,128)} %bitcast.18, f32[200,256]{1,0:T(8,128)} %bitcast.14, ...), custom_call_target="tpu_custom_call" | custom-call | tf_op jit(solution)/shard_map/pallas_call | solution.py:589
  72.4 0.0 copy-start.2
  72.4 0.0 copy-start
  72.4 1.8 %copy.17 = f32[512,200]{0,1:T(8,128)} copy(f32[512,200]{0,1:T(8,128)} %bitcast.13) | data formatting | bytes 819200
  74.2 0.0 copy-done.2
  74.2 0.6 copy.18
  74.8 0.0 copy-done
  74.8 0.0 copy-start.4
  74.8 0.7 copy.19
  75.5 0.0 copy-done.4
  75.5 0.6 copy.20
  (2 shorter events, 0.0 us)
Async XLA Ops:
  0.6 0.7 copy-start.1
  1.3 0.7 copy-start.3
  72.4 1.8 %copy-start.2 = (f32[1,512]{1,0:T(1,128)S(1)}, f32[1,512]{1,0:T(1,128)}, u32[]{:S(2)}) copy-start(f32[1,512]{1,0:T(1,128)} %get-tuple-element.11) | copy-start | bytes 6148
  72.4 2.4 %copy-start = (f32[200,256]{1,0:T(8,128)S(1)}, f32[200,256]{1,0:T(8,128)}, u32[]{:S(2)}) copy-start(f32[200,256]{1,0:T(8,128)} %get-tuple-element.12) | copy-start | bytes 614404
  74.8 0.7 copy-start.4
